TPU v7x, 32 devices: a whole 2x2x4 slice. The times are simulated.
32 devices in a mesh: expert: 16 (over z, y, core), token: 2 (over x).
Axes of the slice: x: 2, y: 2, z: 4, core: 2. Of those that a mesh axis runs over, the one named last changes fastest.
Arguments:
- cotangent: bfloat16 [4096, 2048], P(('expert', 'token')), may hold values from -6 to 6
- expert_ids: int32 [4096, 6], P(('expert', 'token')), may hold values from 0 to 15, all different within a row; in each aligned block of 128 rows (0 to 127, 128 to 255, ...) at most 56 rows name the same one
- gate_values: float32 [4096, 6], P(('expert', 'token')), may hold values from 0.05 to 0.45
- hidden_pre: bfloat16 [16, 1792, 768], P('expert', 'token'), may hold values from -8 to 8
- up_weight: bfloat16 [16, 2048, 768], P('expert'), may hold values from -0.125 to 0.125
- down_weight: bfloat16 [16, 2048, 768], P('expert'), may hold values from -0.21875 to 0.21875
Outputs:
- input_grad: bfloat16 [4096, 2048], P(('expert', 'token'))
- down_grad: bfloat16 [16, 2048, 768], P('expert', 'token')
Inputs may be any that keep to these rules, and one draw needn't show every extreme that they name: `expert_ids`: each row names 6 different experts. Among the 128 rows of one device no expert is named more than 56 times, and in every draw some expert is named exactly 56 times by the rows of some device.
All inputs are finite; a program needn't handle non-finite values.
Results may differ from a plain program's by a relative error of at most 0.007.
Values may be sent and summed in bfloat16 or wider, within the bound.
A program may use at most 128 MiB of HBM per device.

v0:
```python
import functools

import jax
import jax.numpy as jnp
from jax import lax
from jax.experimental import pallas as pl
from jax.experimental.pallas import tpu as pltpu
from jax.sharding import PartitionSpec as P

grad_scale = 0.03125
root_half = 0.7071067811865476
inv_root_two_pi = 0.3989422804014327


def slope_and_act(hidden_rows):
    values = hidden_rows.astype(jnp.float32)
    normal_cdf = 0.5 * (1.0 + lax.erf(values * root_half))
    density = inv_root_two_pi * jnp.exp(-0.5 * values * values)
    slopes = normal_cdf + values * density
    active = (values * normal_cdf).astype(jnp.bfloat16)
    return (slopes, active)


def slot_tables(ids, gates, capacity):
    me = lax.axis_index("expert")
    hit = ids == me
    match = jnp.any(hit, axis=2)
    gate = jnp.sum(jnp.where(hit, gates, 0.0), axis=2)
    rows = ids.shape[1]
    order = jnp.arange(rows, dtype=jnp.int32)
    before = (order[:, None] < order[None, :]).astype(jnp.bfloat16)
    rank = jnp.dot(match.astype(jnp.bfloat16), before, preferred_element_type=jnp.float32)
    rank = jnp.where(match, rank.astype(jnp.int32), -1)
    chosen = rank[:, None, :] == jnp.arange(capacity, dtype=jnp.int32)[None, :, None]
    slot_gate = jnp.sum(jnp.where(chosen, gate[:, None, :], 0.0), axis=2)
    return chosen.astype(jnp.bfloat16), slot_gate


MESH = pl.DeviceIdType.MESH


def ring_place(experts):
    chips = experts // 2
    side = chips // 2
    me = lax.axis_index("expert")
    core = me % 2
    chip = me // 2
    row, odd = chip // 2, chip % 2
    place = row + odd * (chips - 1 - 2 * row)

    def device(at):
        at = (at + 2 * chips) % chips
        back = at // side
        return ((at + back * (chips - 1 - 2 * at)) * 2 + back) * 2

    return place, core, device


def ring_messages(chips):
    side = chips // 2
    return [
        [(d, h) for d in range(1, side + 1) for h in range(2) if d < side or h == way]
        for way in range(2)
    ]


def greet(peers):
    barrier = pltpu.get_barrier_semaphore()
    for peer in peers:
        pl.semaphore_signal(barrier, inc=1, device_id={"expert": peer}, device_id_type=MESH)
    pl.semaphore_wait(barrier, len(peers))


def send(src, dst, send_sem, recv_sem, peer):
    return pltpu.make_async_remote_copy(
        src_ref=src,
        dst_ref=dst,
        send_sem=send_sem,
        recv_sem=recv_sem,
        device_id={"expert": peer},
        device_id_type=MESH,
    )


def gather_kernel(experts, count, *refs):
    mine, outs = refs[:count], refs[count : 2 * count]
    hop_send, hop_recv, sib_send, sib_recv, own_sem, cross_sems = refs[2 * count :]
    chips = experts // 2
    messages = ring_messages(chips)
    place, core, device = ring_place(experts)
    me = lax.axis_index("expert")
    sibling = me + 1 - 2 * core
    peers = (device(place + 1) + core, device(place - 1) + core)
    own = [pltpu.make_async_copy(mine[i], outs[i].at[me], own_sem.at[i]) for i in range(count)]
    for copy in own:
        copy.start()
    greet(peers + (sibling,))

    def rows_of(i, half):
        size = mine[i].shape[0] // 2
        return pl.ds(half * size, size)

    def hop(i, way, index):
        distance, half = messages[way][index]
        sign = 1 - 2 * way
        rows = rows_of(i, half)
        origin = device(place - sign * (distance - 1)) + core
        src = mine[i].at[rows] if distance == 1 else outs[i].at[origin, rows]
        return send(
            src,
            outs[i].at[origin, rows],
            hop_send.at[i, way, index],
            hop_recv.at[i, way, index],
            peers[way],
        )

    def landed(i, way, index, which):
        distance, half = messages[way][index]
        origin = device(place - (1 - 2 * way) * distance) + which
        return outs[i].at[origin, rows_of(i, half)]

    def across(i, way, index, which):
        block = landed(i, way, index, which)
        return send(
            block, block, sib_send.at[i, way, index], sib_recv.at[i, way, index], sibling
        )

    for index in range(2):
        for way in range(2):
            for i in range(count):
                if index < len(messages[way]) and messages[way][index][0] == 1:
                    hop(i, way, index).start()
    cross = [
        send(mine[i], outs[i].at[me], cross_sems.at[0, i], cross_sems.at[1, i], sibling)
        for i in range(count)
    ]
    for copy in cross:
        copy.start()
    for index in range(len(messages[0])):
        for way in range(2):
            distance, half = messages[way][index]
            for i in range(count):
                block = landed(i, way, index, core)
                send(
                    block,
                    block,
                    hop_send.at[i, way, index],
                    hop_recv.at[i, way, index],
                    peers[way],
                ).wait_recv()
                if (distance + 1, half) in messages[way]:
                    hop(i, way, messages[way].index((distance + 1, half))).start()
                across(i, way, index, core).start()
    for i in range(count):
        own[i].wait()
        cross[i].wait_send()
        send(
            mine[i], outs[i].at[sibling], cross_sems.at[0, i], cross_sems.at[1, i], sibling
        ).wait_recv()
        for way in range(2):
            for index in range(len(messages[way])):
                hop(i, way, index).wait_send()
                across(i, way, index, core).wait_send()
                across(i, way, index, 1 - core).wait_recv()


def gather_rows(arrays, name):
    experts = lax.axis_size("expert")
    count = len(arrays)
    steps = len(ring_messages(experts // 2)[0])
    dma = pltpu.SemaphoreType.DMA
    return pl.pallas_call(
        functools.partial(gather_kernel, experts, count),
        out_shape=[jax.ShapeDtypeStruct((experts,) + a.shape, a.dtype) for a in arrays],
        in_specs=[pl.BlockSpec(memory_space=pltpu.VMEM)] * count,
        out_specs=[pl.BlockSpec(memory_space=pl.ANY)] * count,
        scratch_shapes=[
            dma((count, 2, steps)),
            dma((count, 2, steps)),
            dma((count, 2, steps)),
            dma((count, 2, steps)),
            dma((count,)),
            dma((2, count)),
        ],
        compiler_params=pltpu.CompilerParams(
            collective_id=name, has_side_effects=True, vmem_limit_bytes=8 * 1024 * 1024
        ),
        cost_estimate=pl.CostEstimate(
            flops=20_000_000_000, bytes_accessed=20_000_000, transcendentals=0
        ),
        name="gather" + str(name),
    )(*arrays)


def scatter_kernel(
    experts, parts, out, own, other, came, own_sem, sib_send, sib_recv, hop_send, hop_recv
):
    chips = experts // 2
    side = chips // 2
    messages = ring_messages(chips)
    place, core, device = ring_place(experts)
    me = lax.axis_index("expert")
    sibling = me + 1 - 2 * core
    peers = (device(place + 1) + core, device(place - 1) + core)
    size = out.shape[0] // 2
    order = [side]
    for d in range(side - 1, 0, -1):
        order += [d, chips - d]
    order += [0]
    loads = {
        k: pltpu.make_async_copy(parts.at[device(place + k) + core], own.at[k], own_sem.at[k])
        for k in order
    }
    for k in order:
        loads[k].start()
    greet(peers + (sibling,))
    gifts = {
        k: send(
            parts.at[device(place + k) + 1 - core],
            other.at[k],
            sib_send.at[k],
            sib_recv.at[k],
            sibling,
        )
        for k in order
    }
    for k in order:
        gifts[k].start()

    def hop(way, message):
        distance, half = message
        k = distance if way == 0 else chips - distance
        rows = pl.ds(half * size, size)
        index = messages[way].index(message)
        return send(
            own.at[k, rows],
            came.at[way, distance - 1, rows],
            hop_send.at[way, index],
            hop_recv.at[way, index],
            peers[way],
        )

    step = 16

    def add_up(k, half, more, target):
        @pl.loop(0, size // step)
        def _(at):
            rows = pl.ds(pl.multiple_of(half * size + at * step, step), step)
            total = own[k, rows, :].astype(jnp.float32) + other[k, rows, :].astype(jnp.float32)
            for way, slot in more:
                total = total + came[way, slot, rows, :].astype(jnp.float32)
            if target is None:
                own[k, rows, :] = total.astype(own.dtype)
            else:
                target[rows, :] = total.astype(target.dtype)

    ready = set()

    def get(k):
        if k not in ready:
            ready.add(k)
            loads[k].wait()
            gifts[k].wait_recv()

    for distance in range(side, 0, -1):
        for half in range(2):
            for way in range(2):
                if (distance, half) not in messages[way]:
                    continue
                k = distance if way == 0 else chips - distance
                get(k)
                more = []
                if (distance + 1, half) in messages[way]:
                    hop(way, (distance + 1, half)).wait_recv()
                    more = [(way, distance)]
                add_up(k, half, more, None)
                hop(way, (distance, half)).start()
    get(0)
    for half in range(2):
        more = []
        for way in range(2):
            if (1, half) in messages[way]:
                hop(way, (1, half)).wait_recv()
                more.append((way, 0))
        add_up(0, half, more, out)
    for k in order:
        gifts[k].wait_send()
    for way in range(2):
        for message in messages[way]:
            hop(way, message).wait_send()


def scatter_sum(blocks):
    experts, rows, width = blocks.shape
    chips = experts // 2
    steps = len(ring_messages(chips)[0])
    dma = pltpu.SemaphoreType.DMA
    buffers = (3 * chips + 4) * rows * width * 2
    return pl.pallas_call(
        functools.partial(scatter_kernel, experts),
        out_shape=jax.ShapeDtypeStruct((rows, width), blocks.dtype),
        in_specs=[pl.BlockSpec(memory_space=pl.ANY)],
        out_specs=pl.BlockSpec(memory_space=pltpu.VMEM),
        scratch_shapes=[
            pltpu.VMEM((chips, rows, width), blocks.dtype),
            pltpu.VMEM((chips, rows, width), blocks.dtype),
            pltpu.VMEM((2, chips // 2, rows, width), blocks.dtype),
            dma((chips,)),
            dma((chips,)),
            dma((chips,)),
            dma((2, steps)),
            dma((2, steps)),
        ],
        compiler_params=pltpu.CompilerParams(
            collective_id=7, has_side_effects=True, vmem_limit_bytes=buffers + 2 * 1024 * 1024
        ),
        cost_estimate=pl.CostEstimate(
            flops=20_000_000_000, bytes_accessed=20_000_000, transcendentals=0
        ),
        name="scatter_sum",
    )(blocks)


def from_groups(make):
    groups = lax.axis_size("token")
    mine = lax.axis_index("token")
    taken = [make(mine)]
    for shift in range(1, groups):
        pairs = [(t, (t + shift) % groups) for t in range(groups)]
        taken.append(lax.ppermute(make((mine + shift) % groups), "token", pairs))
    return jnp.stack(taken)


def pick(sel, rows):
    return lax.dot_general(
        sel, rows, (((2,), (1,)), ((0,), (0,))), preferred_element_type=jnp.float32
    ).astype(jnp.bfloat16)


def transpose_jacobian(everyone, sel, slot_gate, slopes, up_weight, down_weight):
    blocks, capacity, rows = sel.shape
    picked = pick(sel, everyone).reshape(blocks * capacity, -1)
    inner_prod = jnp.dot(picked, down_weight, preferred_element_type=jnp.float32)
    scaled = (inner_prod * slopes).astype(jnp.bfloat16)
    pieces = lax.dot_general(
        scaled, up_weight, (((1,), (1,)), ((), ())), preferred_element_type=jnp.float32
    ).astype(jnp.bfloat16)
    weighted = (pieces.astype(jnp.float32) * slot_gate.reshape(-1, 1)).astype(jnp.bfloat16)
    spread = lax.dot_general(
        sel,
        weighted.reshape(blocks, capacity, -1),
        (((1,), (1,)), ((0,), (0,))),
        preferred_element_type=jnp.float32,
    ).astype(jnp.bfloat16)
    return scatter_sum(spread)


def body(cotangent, expert_ids, gate_values, hidden_pre, up_weight, down_weight):
    experts = lax.axis_size("expert")
    groups = lax.axis_size("token")
    rows, width = cotangent.shape
    top = expert_ids.shape[1]
    padded = -(-2 * top // 16) * 16
    routes = jnp.concatenate([expert_ids.T.astype(jnp.float32), gate_values.T], axis=0)
    routes = jnp.pad(routes, ((0, padded - 2 * top), (0, 0)))
    routes = from_groups(lambda group: routes).reshape(groups * padded, rows)
    everyone, all_routes = gather_rows([cotangent, routes], 1)
    slopes, active = slope_and_act(hidden_pre[0])
    capacity = slopes.shape[0] // experts
    acts = from_groups(lambda group: active)
    all_routes = all_routes.reshape(experts * groups, padded, rows).transpose(0, 2, 1)
    all_sel, all_gate = slot_tables(
        all_routes[:, :, :top].astype(jnp.int32), all_routes[:, :, top : 2 * top], capacity
    )
    by_group = all_sel.reshape(experts, groups, capacity, rows)
    sel = by_group[:, 0]
    slot_gate = all_gate.reshape(experts, groups, capacity)[:, 0]
    first_term = transpose_jacobian(
        everyone, sel, slot_gate, slopes, up_weight[0], down_weight[0]
    )
    (everyone,) = gather_rows([first_term], 2)
    second = transpose_jacobian(everyone, sel, slot_gate, slopes, up_weight[0], down_weight[0])
    input_grad = (
        cotangent.astype(jnp.float32) + first_term.astype(jnp.float32) + second.astype(jnp.float32)
    ).astype(jnp.bfloat16)
    share = width // groups
    columns = from_groups(
        lambda group: lax.dynamic_slice_in_dim(input_grad, group * share, share, 1)
    ).reshape(groups * rows, share)
    (everyone,) = gather_rows([columns], 3)
    everyone = everyone.reshape(experts * groups, rows, share)
    picked = pick(all_sel, everyone)
    routed = (picked.astype(jnp.float32) * all_gate[:, :, None]).astype(jnp.bfloat16)
    acts = acts.reshape(groups, experts, capacity, -1).transpose(1, 0, 2, 3)
    summed = lax.dot_general(
        routed.reshape(experts * groups * capacity, -1),
        acts.reshape(experts * groups * capacity, -1),
        (((0,), (0,)), ((), ())),
        preferred_element_type=jnp.float32,
    )
    grad_out = (summed * grad_scale).astype(jnp.bfloat16)[None]
    return (input_grad, grad_out)


def solution(mesh):
    in_specs = (
        P(("expert", "token"), None),
        P(("expert", "token"), None),
        P(("expert", "token"), None),
        P("expert", "token", None),
        P("expert", None, None),
        P("expert", None, None),
    )
    out_specs = (P(("expert", "token"), None), P("expert", "token", None))
    return jax.shard_map(body, mesh=mesh, in_specs=in_specs, out_specs=out_specs, check_vma=False)
```

profile of v0, /device:TPU:0, one launch (start us, length us, event | category | flops | bytes accessed | tf_op | source)
XLA Modules:
  0.0 301.4 jit_solution(14363581898544157501)
XLA Ops:
  0.6 0.0 copy-start
  0.6 0.8 convert_bitcast_fusion.1
  1.5 0.8 fusion.48
  2.3 3.0 collective-permute-start
  5.3 2.6 fusion.17
  7.9 0.0 collective-permute-start.2
  7.9 0.0 collective-permute-done
  7.9 1.0 copy-done.3
  8.9 47.1 %gather1.1 = (bf16[16,128,2048]{2,1,0:T(8,128)(2,1)S(1)}, f32[16,32,128]{2,1,0:T(8,128)S(1)}) custom-call(bf16[128,2048]{1,0:T(8,128)(2,1)S(1)} %copy-done.3, f32[32,128]{1,0:T(8,128)S(1)} %bitcast.113), custom_call_target="tpu_custom_call" | custom-call | flops 20000000000 | bytes 20000000 | tf_op jit(solution)/shard_map/gather1/pallas_call | solution.py:172
  56.1 0.0 copy-start.2
  56.1 3.2 %copy-done.2 = bf16[16,128,2048]{2,1,0:T(8,128)(2,1)} copy-done((bf16[16,128,2048]{2,1,0:T(8,128)(2,1)}, bf16[16,128,2048]{2,1,0:T(8,128)(2,1)S(1)}, u32[]{:S(2)}) %copy-start.2) | copy-done | bytes 8388632
  59.3 0.1 fusion.51
  59.4 0.1 fusion.42
  59.4 0.1 fusion.27
  59.6 0.4 select_reduce_fusion
  60.0 0.1 mul.99
  60.1 6.4 %convolution_convert_fusion.3 = bf16[16,56,2048]{2,1,0:T(8,128)(2,1)} fusion(bf16[16,128,2048]{2,1,0:T(8,128)(2,1)} %copy-done.2, s32[16,1,128]{2,0,1:T(8,128)S(1)} %copy.10), kind=kOutput, calls=%fused_computation.14 | convolution fusion | flops 471711744 | bytes 12066816 | tf_op jit(solution)/shard_map/dot_general | solution.py:335
  66.6 0.0 copy-done
  66.6 11.0 %multiply_convert_fusion.2 = bf16[896,2048]{1,0:T(8,128)(2,1)} fusion(f32[896]{0:T(1024)S(1)} %mul.99, bf16[1,2048,768]{2,1,0:T(8,128)(2,1)S(1)} %copy-done, bf16[896,2048]{1,0:T(8,128)(2,1)} %bitcast.115, bf16[1,2048,768]{2,1,0:T(8,128)(2,1)} %param.11, bf16[1,896,768]{2,1,0:T(8,128)(2,1)} %param.9), kind=kOutput, calls=%fused_computation.2 | convolution fusion | flops 5652054016 | bytes 15011328 | tf_op jit(solution)/shard_map/dot_general | solution.py:345
  77.5 4.4 %convolution_convert_fusion.1.parts = bf16[16,128,2048]{2,1,0:T(8,128)(2,1)S(1)} fusion(bf16[16,56,2048]{2,1,0:T(8,128)(2,1)} %bitcast.119, s32[16,1,128]{2,0,1:T(8,128)S(1)} %copy.10), kind=kOutput, calls=%fused_computation.4 | convolution fusion | flops 474071040 | bytes 12066816 | tf_op jit(solution)/shard_map/dot_general | solution.py:349
  82.0 48.7 %scatter_sum.2.refs_0_ = bf16[128,2048]{1,0:T(8,128)(2,1)S(1)} custom-call(bf16[16,128,2048]{2,1,0:T(8,128)(2,1)S(1)} %convolution_convert_fusion.1.parts), custom_call_target="tpu_custom_call" | custom-call | flops 20000000000 | bytes 20000000 | tf_op jit(solution)/shard_map/scatter_sum/pallas_call | solution.py:299
  130.7 0.0 copy-start.5
  130.7 44.9 %gather2.1 = bf16[16,128,2048]{2,1,0:T(8,128)(2,1)S(1)} custom-call(bf16[128,2048]{1,0:T(8,128)(2,1)S(1)} %scatter_sum.2.refs_0_), custom_call_target="tpu_custom_call" | custom-call | flops 20000000000 | bytes 20000000 | tf_op jit(solution)/shard_map/gather2/pallas_call | solution.py:172
  175.6 0.0 copy-done.5
  175.6 3.0 %convolution_convert_fusion.2 = bf16[16,56,2048]{2,1,0:T(8,128)(2,1)} fusion(bf16[16,128,2048]{2,1,0:T(8,128)(2,1)S(1)} %gather2.1, s32[16,1,128]{2,0,1:T(8,128)S(1)} %copy.10), kind=kOutput, calls=%fused_computation.13 | convolution fusion | flops 471711744 | bytes 12066816 | tf_op jit(solution)/shard_map/dot_general | solution.py:335
  178.6 11.0 %multiply_convert_fusion.1 = bf16[896,2048]{1,0:T(8,128)(2,1)} fusion(f32[896]{0:T(1024)S(1)} %mul.99, bf16[1,2048,768]{2,1,0:T(8,128)(2,1)S(1)} %copy-done, bf16[896,2048]{1,0:T(8,128)(2,1)} %bitcast.114, bf16[1,2048,768]{2,1,0:T(8,128)(2,1)} %param.11, bf16[1,896,768]{2,1,0:T(8,128)(2,1)} %param.9), kind=kOutput, calls=%fused_computation.1 | convolution fusion | flops 5652054016 | bytes 15011328 | tf_op jit(solution)/shard_map/dot_general | solution.py:345
  189.6 4.4 %convolution_convert_fusion.parts = bf16[16,128,2048]{2,1,0:T(8,128)(2,1)S(1)} fusion(bf16[16,56,2048]{2,1,0:T(8,128)(2,1)} %bitcast.118, s32[16,1,128]{2,0,1:T(8,128)S(1)} %copy.10), kind=kOutput, calls=%fused_computation.3 | convolution fusion | flops 474071040 | bytes 12066816 | tf_op jit(solution)/shard_map/dot_general | solution.py:349
  194.0 0.0 copy-start.4
  194.1 0.0 copy-start.6
  194.1 47.6 %scatter_sum.3 = bf16[128,2048]{1,0:T(8,128)(2,1)S(1)} custom-call(bf16[16,128,2048]{2,1,0:T(8,128)(2,1)S(1)} %convolution_convert_fusion.parts), custom_call_target="tpu_custom_call" | custom-call | flops 20000000000 | bytes 20000000 | tf_op jit(solution)/shard_map/scatter_sum/pallas_call | solution.py:299
  241.7 0.0 copy-done.4
  241.7 0.0 copy-done.6
  241.7 0.0 copy-start.7
  241.7 0.2 add_convert_fusion
  241.9 0.0 copy-start.8
  242.0 1.6 collective-permute-start.1
  243.6 0.0 copy-done.7
  243.6 0.7 fusion.21
  244.3 5.3 %collective-permute-done.1 = bf16[128,1024]{1,0:T(8,128)(2,1)S(1)} collective-permute-done((bf16[128,1024]{1,0:T(8,128)(2,1)S(1)}, bf16[128,1024]{1,0:T(8,128)(2,1)S(1)}, u32[]{:S(2)}, u32[]{:S(2)}) %collective-permute-start.1) | collective-permute-done | bytes 262176 | tf_op jit(solution)/shard_map/ppermute | solution.py:330
  249.6 0.1 pad_maximum_fusion.1
  249.6 44.6 %gather3.1 = bf16[16,256,1024]{2,1,0:T(8,128)(2,1)S(1)} custom-call(bf16[256,1024]{1,0:T(8,128)(2,1)S(1)} %bitcast.110), custom_call_target="tpu_custom_call" | custom-call | flops 20000000000 | bytes 20000000 | tf_op jit(solution)/shard_map/gather3/pallas_call | solution.py:172
  294.2 0.0 copy-done.8
  294.3 1.2 multiply_convert_fusion
  295.5 0.0 collective-permute-done.2
  295.5 1.6 pad_maximum_fusion
  297.1 0.0 copy-start.1
  297.1 4.2 %fusion.26 = bf16[1,1024,768]{2,1,0:T(8,128)(2,1)} fusion(bf16[1792,1024]{1,0:T(8,128)(2,1)S(1)} %bitcast.117, bf16[1792,768]{1,0:T(8,128)(2,1)S(1)} %bitcast.120), kind=kOutput, calls=%fused_computation.36 | convolution fusion | flops 2820145152 | bytes 7995392 | tf_op jit(solution)/shard_map/dot_general | solution.py:395
  301.4 0.0 copy-done.1
  (6 shorter events, 0.1 us)
Async XLA Ops:
  0.6 65.9 %copy-start = (bf16[1,2048,768]{2,1,0:T(8,128)(2,1)S(1)}, bf16[1,2048,768]{2,1,0:T(8,128)(2,1)}, u32[]{:S(2)}) copy-start(bf16[1,2048,768]{2,1,0:T(8,128)(2,1)} %param.10) | copy-start | bytes 9437188
  2.3 5.6 %collective-permute-start = (f32[16,128]{1,0:T(8,128)S(1)}, f32[16,128]{1,0:T(8,128)S(1)}, u32[]{:S(2)}, u32[]{:S(2)}) collective-permute-start(f32[16,128]{1,0:T(8,128)S(1)} %get-tuple-element.11), channel_id=1, source_target_pairs={{0,1},{1,0},{2,3},{3,2},{4,5},{5,4},{6,7},{7,6},{8,9},{9,8},{10,11... | collective-permute-start | bytes 24584 | tf_op jit(solution)/shard_map/ppermute | solution.py:330
  7.9 287.6 %collective-permute-start.2 = (bf16[896,768]{1,0:T(8,128)(2,1)}, bf16[896,768]{1,0:T(8,128)(2,1)}, u32[]{:S(2)}, u32[]{:S(2)}) collective-permute-start(bf16[896,768]{1,0:T(8,128)(2,1)} %fusion.17), channel_id=1, source_target_pairs={{0,1},{1,0},{2,3},{3,2},{4,5},{5,4},{6,7},{7,6},{8,9},{9,8},{10,11... | collective-permute-start | bytes 4128776 | tf_op jit(solution)/shard_map/ppermute | solution.py:330
  7.9 1.0 copy-start.3
  56.1 3.2 %copy-start.2 = (bf16[16,128,2048]{2,1,0:T(8,128)(2,1)}, bf16[16,128,2048]{2,1,0:T(8,128)(2,1)S(1)}, u32[]{:S(2)}) copy-start(bf16[16,128,2048]{2,1,0:T(8,128)(2,1)S(1)} %get-tuple-element.5) | copy-start | bytes 25165828
  130.7 44.9 %copy-start.5 = (bf16[128,2048]{1,0:T(8,128)(2,1)}, bf16[128,2048]{1,0:T(8,128)(2,1)S(1)}, u32[]{:S(2)}) copy-start(bf16[128,2048]{1,0:T(8,128)(2,1)S(1)} %scatter_sum.2.refs_0_) | copy-start | bytes 1572868
  194.0 47.6 %copy-start.4 = (bf16[128,2048]{1,0:T(8,128)(2,1)S(1)}, bf16[128,2048]{1,0:T(8,128)(2,1)}, u32[]{:S(2)}) copy-start(bf16[128,2048]{1,0:T(8,128)(2,1)} %refs_0_.1) | copy-start | bytes 1572868
  194.1 47.6 %copy-start.6 = (bf16[128,2048]{1,0:T(8,128)(2,1)S(1)}, bf16[128,2048]{1,0:T(8,128)(2,1)}, u32[]{:S(2)}) copy-start(bf16[128,2048]{1,0:T(8,128)(2,1)} %copy-done.5) | copy-start | bytes 1572868
  241.7 1.9 copy-start.7
  241.9 52.3 %copy-start.8 = (bf16[128,2048]{1,0:T(8,128)(2,1)}, bf16[128,2048]{1,0:T(8,128)(2,1)S(1)}, u32[]{:S(2)}) copy-start(bf16[128,2048]{1,0:T(8,128)(2,1)S(1)} %add_convert_fusion) | copy-start | bytes 1572868
  242.0 7.5 %collective-permute-start.1 = (bf16[128,1024]{1,0:T(8,128)(2,1)S(1)}, bf16[128,1024]{1,0:T(8,128)(2,1)S(1)}, u32[]{:S(2)}, u32[]{:S(2)}) collective-permute-start(bf16[128,1024]{1,0:T(8,128)(2,1)S(1)} %get-tuple-element.9), channel_id=1, source_target_pairs={{0,1},{1,0},{2,3},{3,2},{4,5},{5,4},{6,7},{7,6},{8,9},{9,8},{10,11... | collective-permute-start | bytes 786440 | tf_op jit(solution)/shard_map/ppermute | solution.py:330
  297.1 4.3 %copy-start.1 = (bf16[1,2048,768]{2,1,0:T(8,128)(2,1)S(1)}, bf16[1,2048,768]{2,1,0:T(8,128)(2,1)}, u32[]{:S(2)}) copy-start(bf16[1,2048,768]{2,1,0:T(8,128)(2,1)} %param.10) | copy-start | bytes 9437188
where the time goes:
time: 302 us; the launch traced here: 301 us
  Pallas kernels  233 us (77%)
  matrix products  45.9 us (15%)
  other arithmetic  7.33 us (2%)
  waiting for transfers between devices  5.3 us (2%)
  starting transfers between devices  4.55 us (2%)
  local copies, waits for them, and re-layouts  4.46 us (1%)
    pallas_call x3, Pallas kernels, gather_rows(): pl.pallas_call(functools.partial(gather_kernel, experts, count), out_shap...  137 us
    pallas_call x2, Pallas kernels, scatter_sum(): pl.pallas_call(functools.partial(scatter_kernel, experts), out_shape=jax....  96.3 us
    dot_general x2, matrix products, transpose_jacobian(): lax.dot_general(scaled, up_weight, (((1,), (1,)), ((), ())), preferred_el...  22 us
    dot_general x3, matrix products, pick(): lax.dot_general(sel, rows, (((2,), (1,)), ((0,), (0,))), preferred_elemen...  10.7 us
    dot_general x2, matrix products, transpose_jacobian(): lax.dot_general(sel, weighted.reshape(blocks, capacity, -1), (((1,), (1,)...  8.87 us
  transfers between devices with their start and end apart: 3, of which 1 were waited for; matrix products, arithmetic and copies ran while one was open for 15% of the time, Pallas kernels for 77%

commit v1 on v0

--- a/solution.py
+++ b/solution.py
@@ -355,7 +355,7 @@
     return scatter_sum(spread)
 
 
-def body(cotangent, expert_ids, gate_values, hidden_pre, up_weight, down_weight):
+def staged(cotangent, expert_ids, gate_values, hidden_pre, up_weight, down_weight):
     experts = lax.axis_size("expert")
     groups = lax.axis_size("token")
     rows, width = cotangent.shape
@@ -402,6 +402,693 @@
     return (input_grad, grad_out)
 
 
+class Plan:
+    def __init__(self, experts, groups, rows, width, hidden, slots):
+        self.experts, self.groups, self.rows, self.width = experts, groups, rows, width
+        self.hidden, self.slots = hidden, slots
+        self.capacity = slots // experts
+        self.planes = experts // 4
+        self.chains = 2
+        self.n = rows // self.chains
+        self.split = width * 5 // 8 // 128 * 128
+
+    def fits(self):
+        lanes = 128
+        whole = (
+            self.groups == 2
+            and self.experts % 4 == 0
+            and 2 * self.experts <= lanes
+            and self.planes <= 4
+            and self.rows == lanes
+            and self.n % 16 == 0
+            and self.width % (4 * lanes) == 0
+            and self.hidden % (2 * lanes) == 0
+            and (2 * self.capacity) % 16 == 0
+            and 2 * self.capacity <= 2 * lanes
+            and self.slots <= self.rows * self.experts // self.chains
+            and self.hidden <= self.width
+        )
+        return whole and self.bytes() <= 63 * 1024 * 1024
+
+    def bytes(self):
+        e, r, d, h, z = self.experts, self.rows, self.width, self.hidden, self.planes
+        tokens = 2 * e * r * d * 2 + e * r * d * 2 + e * r * d
+        lines = self.chains * (2 * z * self.n * (2 * d - self.split) + z * self.n * self.split) * 2
+        return tokens + lines + 2 * d * h * 2 + e * r * h * (4 + 2 + 2) + 3 * r * d * 2 + d * h * 2 + d * h
+
+    def semaphores(self):
+        return self.chains * 34 * self.planes + 16 * self.planes
+
+
+def fused_kernel(
+    plan,
+    cot,
+    ids,
+    gates,
+    hidden_hbm,
+    up_hbm,
+    down_hbm,
+    grad_in,
+    grad_w,
+    view,
+    part,
+    gift,
+    came,
+    came2,
+    rung,
+    last,
+    slope,
+    act,
+    other,
+    first,
+    third,
+    tabs,
+    own_tab,
+    turn,
+    scaled,
+    up,
+    down,
+    total,
+    send_sems,
+    recv_sems,
+    load_sems,
+):
+    experts, planes, chains, n = plan.experts, plan.planes, plan.chains, plan.n
+    width, hidden, cap, split = plan.width, plan.hidden, plan.capacity, plan.split
+    top = ids.shape[1]
+    half = width // 2
+    rest = width - split
+    me = lax.axis_index("expert")
+    token = lax.axis_index("token")
+    core = me % 2
+    y = (me // 2) % 2
+    z = me // 4
+    has = {0: z > 0, 1: z < planes - 1}
+    up_peer = {"expert": me + 4}
+    down_peer = {"expert": me - 4}
+    rung_peer = {"expert": me + 2 - 4 * y}
+    sib_peer = {"expert": me + 1 - 2 * core}
+    far_peer = {"token": 1 - token}
+    sources = ((0, up_peer), (1, down_peer))
+    c1, c2, full = pl.ds(0, split), pl.ds(split, rest), pl.ds(0, width)
+
+    keys = {}
+
+    def number(key):
+        if key not in keys:
+            keys[key] = len(keys)
+            assert len(keys) <= plan.semaphores()
+        return keys[key]
+
+    def copy(key, src, dst, peer):
+        at = number(key)
+        return pltpu.make_async_remote_copy(
+            src_ref=src,
+            dst_ref=dst,
+            send_sem=send_sems.at[at],
+            recv_sem=recv_sems.at[at],
+            device_id=peer,
+            device_id_type=MESH,
+        )
+
+    def when(cond, action):
+        if cond is None:
+            action()
+        else:
+            pl.when(cond)(action)
+
+    pending = {}
+
+    def post(group, cond, key, src, dst, peer):
+        when(cond, lambda: copy(key, src, dst, peer).start())
+        pending.setdefault(group, []).append((cond, key, src, peer))
+
+    def drain(group):
+        for cond, key, src, peer in pending.pop(group, []):
+            when(cond, lambda: copy(key, src, src, peer).wait_send())
+
+    def arrive(cond, key, dst):
+        when(cond, lambda: copy(key, dst, dst, sib_peer).wait_recv())
+
+    def both(a, b):
+        return b if a is None else (a if b is None else jnp.logical_and(a, b))
+
+    def slot_of(p, yy, cc):
+        return 4 * p + 2 * cc + yy
+
+    def origin(way, d):
+        return z - d if way == 0 else z + d
+
+    def there(way, d):
+        return z >= d if way == 0 else z + d < planes
+
+    mine = slot_of(z, y, core)
+    beside = slot_of(z, 1 - y, core)
+
+    def gather(tag, at, src, whole):
+        group = ("ag", tag)
+
+        def start():
+            drain(group)
+            post(group, None, (tag, "rung"), src, at(mine, full), rung_peer)
+            for way, peer in sources:
+                post(group, has[1 - way], (tag, "rail", way, 1), src, at(mine, full), peer)
+            post(group, None, (tag, "sib"), src, at(mine, full), sib_peer)
+
+        def step(d):
+            if d == 0:
+                block = at(beside, full)
+                arrive(None, (tag, "rung"), block)
+                if not whole:
+                    cut = at(beside, c2)
+                    for way, peer in sources:
+                        post(group, has[1 - way], (tag, "rail2", way, 1), cut, cut, peer)
+                post(group, None, (tag, "sibp"), block, block, sib_peer)
+                return
+            for way, peer in sources:
+                cond = there(way, d)
+                o = slot_of(origin(way, d), y, core)
+                block = at(o, full)
+                arrive(cond, (tag, "rail", way, d), block)
+                if d + 1 < planes:
+                    on = both(cond, has[1 - way])
+                    post(group, on, (tag, "rail", way, d + 1), block, block, peer)
+                over = block if whole else at(o, c1)
+                post(group, cond, (tag, "over", way, d), over, over, rung_peer)
+                post(group, cond, (tag, "sib", way, d), block, block, sib_peer)
+            if whole:
+                return
+            for way, peer in sources:
+                cond = there(way, d)
+                cut = at(slot_of(origin(way, d), 1 - y, core), c2)
+                arrive(cond, (tag, "rail2", way, d), cut)
+                if d + 1 < planes:
+                    on = both(cond, has[1 - way])
+                    post(group, on, (tag, "rail2", way, d + 1), cut, cut, peer)
+                post(group, cond, (tag, "sib2", way, d), cut, cut, sib_peer)
+
+        def across(d):
+            for way in range(2):
+                cond = there(way, d)
+                cut = at(slot_of(origin(way, d), 1 - y, core), full if whole else c1)
+                arrive(cond, (tag, "over", way, d), cut)
+                post(group, cond, (tag, "sib1", way, d), cut, cut, sib_peer)
+
+        def ready(d):
+            if d == 0:
+                arrive(None, (tag, "sib"), at(slot_of(z, y, 1 - core), full))
+                arrive(None, (tag, "sibp"), at(slot_of(z, 1 - y, 1 - core), full))
+                return
+            for way in range(2):
+                cond = there(way, d)
+                p = origin(way, d)
+                arrive(cond, (tag, "sib", way, d), at(slot_of(p, y, 1 - core), full))
+                o = slot_of(p, 1 - y, 1 - core)
+                if not whole:
+                    arrive(cond, (tag, "sib2", way, d), at(o, c2))
+                arrive(cond, (tag, "sib1", way, d), at(o, full if whole else c1))
+
+        return start, step, across, ready
+
+    def plane_at(i):
+        low = jnp.minimum(z, planes - 1 - z)
+        near = jnp.where(z < planes // 2, 1, -1)
+        d = jnp.where(i <= 2 * low, (i + 1) // 2, i - low)
+        sign = jnp.where(i <= 2 * low, near * (1 if i % 2 else -1), near)
+        return z + sign * d if i else z
+
+    tab_at = lambda slot, cols: tabs.at[slot]
+    tab_start, tab_step, tab_across, tab_ready = gather("tab", tab_at, own_tab, True)
+
+    sources_of = {0: cot, 1: first, 2: third}
+
+    def chain_rows(chain):
+        return pl.ds(chain * n, n)
+
+    stages = {}
+    for chain in range(chains):
+        for f in range(3):
+
+            def at(slot, cols, f=f, chain=chain):
+                rows = pl.ds(pl.multiple_of(slot * n, n), n)
+                return view.at[f % 2, chain, rows, cols]
+
+            src = sources_of[f].at[chain_rows(chain)]
+            stages[f, chain] = gather(chain, at, src, False)
+
+    def start(f, chain):
+        stages[f, chain][0]()
+        rows = pl.ds(pl.multiple_of(mine * n, n), n)
+        view[f % 2, chain, rows, :] = sources_of[f][chain_rows(chain), :]
+
+    def hop(f, chain, d):
+        stages[f, chain][1](d)
+
+    def over(f, chain, d):
+        if d:
+            stages[f, chain][2](d)
+        stages[f, chain][3](d)
+
+    hidden_at = view.at[1, 0, pl.ds(0, plan.slots), pl.ds(0, hidden)]
+    loads = [
+        pltpu.make_async_copy(hidden_hbm, hidden_at, load_sems.at[0]),
+        pltpu.make_async_copy(down_hbm, down, load_sems.at[1]),
+        pltpu.make_async_copy(up_hbm, up, load_sems.at[2]),
+    ]
+
+    def make_table():
+        lanes = plan.rows
+        shape = (plan.rows, lanes)
+        lane = lax.broadcasted_iota(jnp.int32, shape, 1)
+        row = lax.broadcasted_iota(jnp.int32, shape, 0)
+        match = jnp.zeros(shape, jnp.float32)
+        gate = jnp.zeros(shape, jnp.float32)
+        for k in range(top):
+            name = ids[:, k : k + 1]
+            match = match + jnp.where(name == lane, 1.0, 0.0)
+            gate = gate + jnp.where(name + experts == lane, gates[:, k : k + 1], 0.0)
+        before = jnp.where(lane < row, 1.0, 0.0).astype(jnp.bfloat16)
+        rank = jnp.dot(before, match.astype(jnp.bfloat16), preferred_element_type=jnp.float32)
+        rank = jnp.where(match > 0.5, rank, -4.0 * lanes)
+        table = jnp.where(lane < experts, rank, gate).T
+        own_tab[...] = table[: 2 * experts, :]
+        tabs[mine] = table[: 2 * experts, :]
+
+    tile = 256
+
+    def prepare(i):
+        p = plane_at(i)
+        for j in range(4):
+            turn[pl.ds(j, 1), :] = tabs[4 * p + j, pl.ds(me, 1), :]
+            turn[pl.ds(4 + j, 1), :] = tabs[4 * p + j, pl.ds(experts + me, 1), :]
+        turned = turn[...].T
+        spot = lax.broadcasted_iota(jnp.int32, (plan.rows, 2 * cap), 1).astype(jnp.float32)
+
+        @pl.loop(0, hidden // tile)
+        def _(step):
+            cols = pl.ds(pl.multiple_of(step * tile, tile), tile)
+            for yy in range(2):
+                rows = pl.ds(pl.multiple_of((4 * p + 2 * yy) * cap, 2 * cap), 2 * cap)
+                values = view[1, 0, rows, cols].astype(jnp.float32)
+                normal_cdf = 0.5 * (1.0 + lax.erf(values * root_half))
+                density = inv_root_two_pi * jnp.exp(-0.5 * values * values)
+                steep = normal_cdf + values * density
+                active = (values * normal_cdf).astype(jnp.bfloat16)
+                high = steep.astype(jnp.bfloat16)
+                low = (steep - high.astype(jnp.float32)).astype(jnp.bfloat16)
+                for cc in range(2):
+                    j = 2 * cc + yy
+                    sel = jnp.where(turned[:, j : j + 1] + float(cc * cap) == spot, 1.0, 0.0)
+                    sel = sel.astype(jnp.bfloat16)
+                    gate = turned[:, 4 + j : 5 + j]
+                    pick = lambda rhs: jnp.dot(sel, rhs, preferred_element_type=jnp.float32)
+                    steeps = (pick(high) + pick(low)) * gate
+                    actives = (pick(active) * gate).astype(jnp.bfloat16)
+                    for chain in range(chains):
+                        to = pl.ds(pl.multiple_of((4 * p + j) * n, n), n)
+                        slope[chain, to, cols] = steeps[chain * n : (chain + 1) * n]
+                        act[chain, to, cols] = actives[chain * n : (chain + 1) * n]
+
+    unit_rows = 4 * n
+
+    def apply(f, chain, i):
+        p = plane_at(i)
+        rows = pl.ds(pl.multiple_of(p * unit_rows, unit_rows), unit_rows)
+        if i == 0:
+            drain(("rs", chain))
+
+        @pl.loop(0, hidden // tile)
+        def _(step):
+            cols = pl.ds(pl.multiple_of(step * tile, tile), tile)
+            inner = jnp.dot(
+                view[f % 2, chain, rows, :], down[:, cols], preferred_element_type=jnp.float32
+            )
+            scaled[:, cols] = (inner * slope[chain, rows, cols]).astype(jnp.bfloat16)
+
+        wide = 2 * tile
+
+        @pl.loop(0, width // wide)
+        def _(step):
+            cols = pl.ds(pl.multiple_of(step * wide, wide), wide)
+            piece = lax.dot_general(
+                scaled[...],
+                up[cols, :],
+                (((1,), (1,)), ((), ())),
+                preferred_element_type=jnp.float32,
+            )
+            part[chain, rows, cols] = piece.astype(jnp.bfloat16)
+
+        away = pl.ds(pl.multiple_of(p * unit_rows + (1 - core) * 2 * n, 2 * n), 2 * n)
+        post(
+            ("rs", chain),
+            None,
+            ("gift", chain, i),
+            part.at[chain, away],
+            gift.at[chain, p],
+            sib_peer,
+        )
+
+    def part_rows(p, yy):
+        return pl.multiple_of(slot_of(p, yy, core) * n, n)
+
+    chunk = 16
+
+    def add_up(terms, store):
+        @pl.loop(0, n // chunk)
+        def _(step):
+            start = pl.multiple_of(step * chunk, chunk)
+            value = None
+            for term in terms:
+                x = term(start).astype(jnp.float32)
+                value = x if value is None else value + x
+            store(start, value)
+
+    def from_part(chain, p, yy, cols):
+        base = part_rows(p, yy)
+        return lambda s: part[chain, pl.ds(pl.multiple_of(base + s, chunk), chunk), cols]
+
+    def to_part(chain, p, yy, cols):
+        base = part_rows(p, yy)
+
+        def store(s, value):
+            rows = pl.ds(pl.multiple_of(base + s, chunk), chunk)
+            part[chain, rows, cols] = value.astype(jnp.bfloat16)
+
+        return store
+
+    def from_gift(chain, p, yy, cols):
+        base = pl.multiple_of(yy * n, n)
+        return lambda s: gift[chain, p, pl.ds(pl.multiple_of(base + s, chunk), chunk), cols]
+
+    def rows_at(s):
+        return pl.ds(s, chunk)
+
+    def lend(chain, i):
+        p = plane_at(i)
+        arrive(None, ("gift", chain, i), gift.at[chain, p])
+        add_up(
+            [from_part(chain, p, 1 - y, full), from_gift(chain, p, 1 - y, full)],
+            to_part(chain, p, 1 - y, full),
+        )
+        src = part.at[chain, pl.ds(part_rows(p, 1 - y), n), c1]
+        post(("rs", chain), None, ("lend", chain, i), src, rung.at[chain, p], rung_peer)
+
+    def lent(chain, i):
+        arrive(None, ("lend", chain, i), rung.at[chain, plane_at(i)])
+
+    def carry(chain, d):
+        for way, peer in sources:
+            to = z + d if way == 0 else z - d
+            cond = there(1 - way, d)
+            more = both(cond, has[way])
+
+            @pl.when(cond)
+            def _():
+                group = ("rs", chain)
+                if d + 1 < planes:
+                    arrive(more, ("rs2", chain, way, d + 1), came2.at[chain, way, to])
+                add_up(
+                    [
+                        from_part(chain, to, 1 - y, c2),
+                        lambda s: came2[chain, way, to, rows_at(s), :],
+                    ],
+                    to_part(chain, to, 1 - y, c2),
+                )
+                src = part.at[chain, pl.ds(part_rows(to, 1 - y), n), c2]
+                copy(("rs2", chain, way, d), src, came2.at[chain, way, to], peer).start()
+                if d + 1 < planes:
+                    arrive(more, ("rs", chain, way, d + 1), came.at[chain, way, to])
+                add_up(
+                    [
+                        from_part(chain, to, y, c1),
+                        from_gift(chain, to, y, c1),
+                        lambda s: rung[chain, to, rows_at(s), :],
+                        lambda s: came[chain, way, to, rows_at(s), c1],
+                    ],
+                    to_part(chain, to, y, c1),
+                )
+                add_up(
+                    [
+                        from_part(chain, to, y, c2),
+                        from_gift(chain, to, y, c2),
+                        lambda s: came[chain, way, to, rows_at(s), c2],
+                    ],
+                    to_part(chain, to, y, c2),
+                )
+                src = part.at[chain, pl.ds(part_rows(to, y), n)]
+                copy(("rs", chain, way, d), src, came.at[chain, way, to], peer).start()
+
+            group = ("rs", chain)
+            src2 = part.at[chain, pl.ds(part_rows(to, 1 - y), n), c2]
+            src1 = part.at[chain, pl.ds(part_rows(to, y), n)]
+            pending.setdefault(group, []).append((cond, ("rs2", chain, way, d), src2, peer))
+            pending.setdefault(group, []).append((cond, ("rs", chain, way, d), src1, peer))
+
+    def settle2(chain):
+        for way in range(2):
+            arrive(has[way], ("rs2", chain, way, 1), came2.at[chain, way, z])
+        add_up(
+            [from_part(chain, z, 1 - y, c2)]
+            + [lambda s, way=way: came2[chain, way, z, rows_at(s), :] for way in range(2)],
+            to_part(chain, z, 1 - y, c2),
+        )
+        src = part.at[chain, pl.ds(part_rows(z, 1 - y), n), c2]
+        post(("rs", chain), None, ("last", chain), src, last.at[chain], rung_peer)
+
+    def settle(f, chain):
+        for way in range(2):
+            arrive(has[way], ("rs", chain, way, 1), came.at[chain, way, z])
+
+        def finish(cols):
+            def store(s, value):
+                rows = pl.ds(pl.multiple_of(chain * n + s, chunk), chunk)
+                term = value.astype(jnp.bfloat16)
+                if f == 0:
+                    first[rows, cols] = term
+                else:
+                    whole = (
+                        cot[rows, cols].astype(jnp.float32)
+                        + first[rows, cols].astype(jnp.float32)
+                        + term.astype(jnp.float32)
+                    )
+                    grad_in[rows, cols] = whole.astype(jnp.bfloat16)
+
+            return store
+
+        sides = [lambda s, way=way: came[chain, way, z, rows_at(s), c1] for way in range(2)]
+        add_up(
+            [
+                from_part(chain, z, y, c1),
+                from_gift(chain, z, y, c1),
+                lambda s: rung[chain, z, rows_at(s), :],
+            ]
+            + sides,
+            finish(c1),
+        )
+        arrive(None, ("last", chain), last.at[chain])
+        sides = [lambda s, way=way: came[chain, way, z, rows_at(s), c2] for way in range(2)]
+        add_up(
+            [
+                from_part(chain, z, y, c2),
+                from_gift(chain, z, y, c2),
+                lambda s: last[chain, rows_at(s), :],
+            ]
+            + sides,
+            finish(c2),
+        )
+
+    def swap(chain):
+        rows = chain_rows(chain)
+        away = pl.ds(pl.multiple_of((1 - token) * half, half), half)
+        keep = pl.ds(pl.multiple_of(token * half, half), half)
+        post(
+            "swap",
+            None,
+            ("swap", chain),
+            grad_in.at[rows, away],
+            third.at[rows, pl.ds(half, half)],
+            far_peer,
+        )
+        third[rows, pl.ds(0, half)] = grad_in[rows, keep]
+
+    def swapped(chain):
+        arrive(None, ("swap", chain), third.at[chain_rows(chain), pl.ds(half, half)])
+
+    def weigh(chain, i, begin, end):
+        p = plane_at(i)
+        rows = pl.ds(pl.multiple_of(p * unit_rows, unit_rows), unit_rows)
+
+        @pl.loop(0, half // tile)
+        def _(step):
+            base = pl.multiple_of(step * tile, tile)
+            out = pl.ds(base, tile)
+            dims = (((0,), (0,)), ((), ()))
+            value = lax.dot_general(
+                view[0, chain, rows, pl.ds(base, tile)],
+                act[chain, rows, :],
+                dims,
+                preferred_element_type=jnp.float32,
+            )
+            value = value + lax.dot_general(
+                view[0, chain, rows, pl.ds(pl.multiple_of(half + base, tile), tile)],
+                other[chain, rows, :],
+                dims,
+                preferred_element_type=jnp.float32,
+            )
+            if not begin:
+                value = value + total[out, :]
+            if end:
+                grad_w[out, :] = (value * grad_scale).astype(jnp.bfloat16)
+            else:
+                total[out, :] = value
+
+    for load in loads:
+        load.start()
+    barrier = pltpu.get_barrier_semaphore()
+    for cond, peer in (
+        (has[1], up_peer),
+        (has[0], down_peer),
+        (None, rung_peer),
+        (None, sib_peer),
+        (None, far_peer),
+    ):
+        when(
+            cond,
+            lambda: pl.semaphore_signal(barrier, inc=1, device_id=peer, device_id_type=MESH),
+        )
+    make_table()
+    turn[...] = jnp.zeros_like(turn)
+    for way in range(2):
+
+        @pl.when(jnp.logical_not(has[way]))
+        def _():
+            for chain in range(chains):
+                came[chain, way] = jnp.zeros(came.shape[2:], came.dtype)
+                came2[chain, way] = jnp.zeros(came2.shape[2:], came2.dtype)
+
+    count = 3 + jnp.where(z > 0, 1, 0) + jnp.where(z < planes - 1, 1, 0)
+    pl.semaphore_wait(barrier, count)
+
+    last_step = planes - 1
+    tab_start()
+    start(0, 0)
+    tab_step(0)
+    for load in loads:
+        load.wait()
+    for d in range(planes):
+        if d:
+            tab_step(d)
+            tab_across(d)
+        hop(0, 0, d)
+        tab_ready(d)
+        prepare(d)
+        over(0, 0, d)
+        if d == 0:
+            start(0, 1)
+        apply(0, 0, d)
+    post("act", None, "act", act, other, far_peer)
+
+    def slot(f, a, g, b, begin, unit):
+        if begin:
+            begin()
+        lend(b, last_step)
+        for d in range(planes):
+            hop(f, a, d)
+            if d < last_step:
+                lend(b, last_step - 1 - d)
+                lent(b, last_step - d)
+                carry(b, last_step - d)
+            over(f, a, d)
+            unit(a, d)
+        lent(b, 0)
+        settle2(b)
+        settle(g, b)
+
+    slot(0, 1, 0, 0, None, lambda a, i: apply(0, a, i))
+    slot(1, 0, 0, 1, lambda: start(1, 0), lambda a, i: apply(1, a, i))
+    slot(1, 1, 1, 0, lambda: start(1, 1), lambda a, i: apply(1, a, i))
+    swap(0)
+    arrive(None, "act", other)
+    swapped(0)
+    slot(2, 0, 1, 1, lambda: start(2, 0), lambda a, i: weigh(a, i, i == 0, False))
+    swap(1)
+    swapped(1)
+    start(2, 1)
+    for d in range(planes):
+        hop(2, 1, d)
+        over(2, 1, d)
+        weigh(1, d, False, d == last_step)
+    for group in list(pending):
+        drain(group)
+
+
+def fused(plan, cotangent, expert_ids, gate_values, hidden_pre, up_weight, down_weight):
+    experts, planes, chains, n = plan.experts, plan.planes, plan.chains, plan.n
+    width, hidden, rows = plan.width, plan.hidden, plan.rows
+    half = width // 2
+    low, dma = jnp.bfloat16, pltpu.SemaphoreType.DMA
+    vmem = pl.BlockSpec(memory_space=pltpu.VMEM)
+    hbm = pl.BlockSpec(memory_space=pl.ANY)
+    count = plan.semaphores()
+    return pl.pallas_call(
+        functools.partial(fused_kernel, plan),
+        out_shape=[
+            jax.ShapeDtypeStruct((rows, width), low),
+            jax.ShapeDtypeStruct((half, hidden), low),
+        ],
+        in_specs=[vmem, vmem, vmem, hbm, hbm, hbm],
+        out_specs=[vmem, vmem],
+        scratch_shapes=[
+            pltpu.VMEM((2, chains, experts * n, width), low),
+            pltpu.VMEM((chains, experts * n, width), low),
+            pltpu.VMEM((chains, planes, 2 * n, width), low),
+            pltpu.VMEM((chains, 2, planes, n, width), low),
+            pltpu.VMEM((chains, 2, planes, n, width - plan.split), low),
+            pltpu.VMEM((chains, planes, n, plan.split), low),
+            pltpu.VMEM((chains, n, width - plan.split), low),
+            pltpu.VMEM((chains, experts * n, hidden), jnp.float32),
+            pltpu.VMEM((chains, experts * n, hidden), low),
+            pltpu.VMEM((chains, experts * n, hidden), low),
+            pltpu.VMEM((rows, width), low),
+            pltpu.VMEM((rows, width), low),
+            pltpu.VMEM((experts, 2 * experts, rows), jnp.float32),
+            pltpu.VMEM((2 * experts, rows), jnp.float32),
+            pltpu.VMEM((rows, rows), jnp.float32),
+            pltpu.VMEM((4 * n, hidden), low),
+            pltpu.VMEM((width, hidden), low),
+            pltpu.VMEM((width, hidden), low),
+            pltpu.VMEM((half, hidden), jnp.float32),
+            dma((count,)),
+            dma((count,)),
+            dma((3,)),
+        ],
+        compiler_params=pltpu.CompilerParams(
+            collective_id=5, has_side_effects=True, vmem_limit_bytes=67_043_328
+        ),
+        cost_estimate=pl.CostEstimate(
+            flops=40_000_000_000, bytes_accessed=20_000_000, transcendentals=0
+        ),
+        name="fused",
+    )(cotangent, expert_ids, gate_values, hidden_pre, up_weight, down_weight)
+
+
+def body(cotangent, expert_ids, gate_values, hidden_pre, up_weight, down_weight):
+    plan = Plan(
+        lax.axis_size("expert"),
+        lax.axis_size("token"),
+        cotangent.shape[0],
+        cotangent.shape[1],
+        hidden_pre.shape[2],
+        hidden_pre.shape[1],
+    )
+    if not plan.fits():
+        return staged(cotangent, expert_ids, gate_values, hidden_pre, up_weight, down_weight)
+    input_grad, grad_out = fused(
+        plan, cotangent, expert_ids, gate_values, hidden_pre[0], up_weight[0], down_weight[0]
+    )
+    return (input_grad, grad_out[None])
+
+
 def solution(mesh):
     in_specs = (
         P(("expert", "token"), None),

time: 302 us -> 293 us (0.970)
  Pallas kernels: 233 us -> 285 us
  matrix products: 45.9 us -> 0 us
  other arithmetic: 7.33 us -> 0 us
  waiting for transfers between devices: 5.3 us -> 0 us
  starting transfers between devices: 4.55 us -> 0 us
    pallas_call x5 -> x1, Pallas kernels: 233 us -> 285 us  [fused(): pl.pallas_call(functools.partial(fused_kernel, plan), out_shape=[jax.Shap...]
    dot_general x9 -> x0, matrix products: 45.9 us -> none  [the longest x2 22 us: transpose_jacobian(): lax.dot_general(scaled, up_weight, (((1,), (1,)), ((), ())), preferred_el...]
    ppermute x3 -> x0, waiting for transfers between devices: 5.3 us -> none  [from_groups(): taken.append(lax.ppermute(make((mine + shift) % groups), 'token', pairs))]
    ppermute x3 -> x0, starting transfers between devices: 4.55 us -> none  [from_groups(): taken.append(lax.ppermute(make((mine + shift) % groups), 'token', pairs))]
    convert_element_type x4 -> x0, other arithmetic: 4.35 us -> none  [the longest x2 3.27 us: slope_and_act(): active = (values * normal_cdf).astype(jnp.bfloat16)]
    unnamed x19 -> x4, local copies, waits for them, and re-layouts: 4.3 us -> 7.37 us
  transfers between devices with their start and end apart: 3 -> 0, of which waited for: 1 -> 0; matrix products, arithmetic and copies ran while one was open for 15% -> 0% of each run, Pallas kernels for 77% -> 0%
where the time goes in v1:
time: 293 us
  Pallas kernels  285 us (97%)
  local copies, waits for them, and re-layouts  7.37 us (3%)
    pallas_call x1, Pallas kernels, fused(): pl.pallas_call(functools.partial(fused_kernel, plan), out_shape=[jax.Shap...  285 us
    unnamed x4, local copies, waits for them, and re-layouts  7.37 us

profile of v1, /device:TPU:0, one launch (start us, length us, event | category | flops | bytes accessed | tf_op | source)
XLA Modules:
  0.0 293.2 jit_solution(2591626181291172931)
XLA Ops:
  0.6 1.4 copy.8.ids
  2.1 1.4 copy.9.gates
  3.5 285.2 %fused.1 = (bf16[128,2048]{1,0:T(8,128)(2,1)}, bf16[1024,768]{1,0:T(8,128)(2,1)}) custom-call(bf16[128,2048]{1,0:T(8,128)(2,1)} %cot.1, s32[128,6]{1,0:T(8,128)} %copy.8.ids, f32[128,6]{1,0:T(8,128)} %copy.9.gates, bf16[896,768]{1,0:T(8,128)(2,1)} %bitcast.7, bf16[2048,768]{1,0:T(8,128)(2,1)} %bitcast.5, bf16[2048,768]{1,0:T(8,128)(2,1)} %bitcast.6), custom_call_target="tpu_custom_call" | custom-call | flops 40000000000 | bytes 20000000 | tf_op jit(solution)/shard_map/fused/pallas_call | solution.py:1033
  288.7 1.9 copy.12
  290.6 2.7 copy.13

commit v2 on v0

--- a/solution.py
+++ b/solution.py
@@ -355,7 +355,7 @@
     return scatter_sum(spread)
 
 
-def body(cotangent, expert_ids, gate_values, hidden_pre, up_weight, down_weight):
+def staged(cotangent, expert_ids, gate_values, hidden_pre, up_weight, down_weight):
     experts = lax.axis_size("expert")
     groups = lax.axis_size("token")
     rows, width = cotangent.shape
@@ -402,6 +402,877 @@
     return (input_grad, grad_out)
 
 
+NAMES = ("aS", "aH0", "aH", "aK", "aO", "aR", "tS", "tH0", "tH", "tO", "tR")
+NAMES += ("P", "X", "N", "U", "L", "D", "C", "T2", "T1", "T", "W")
+ORDER = (
+    (6, 0, 0), (0, 0, 0), (0, 0, 1), (8, 0, 0, 1, 0), (1, 0, 0), (8, 0, 0, 1, 1), (2, 0, 0, 1, 0),
+    (2, 0, 0, 1, 1), (8, 0, 0, 2, 0), (12, 0), (7, 0, 0), (8, 0, 0, 2, 1), (2, 0, 1, 1, 0),
+    (2, 0, 1, 1, 1), (2, 0, 0, 2, 1), (3, 0, 0, 1, 1), (10, 0, 0, 0), (9, 0, 0, 1, 1),
+    (9, 0, 0, 1, 0), (2, 0, 0, 2, 0), (11, 0), (10, 0, 0, 1), (1, 0, 1), (12, 1), (9, 0, 0, 2, 1),
+    (3, 0, 0, 1, 0), (8, 0, 0, 3, 1), (9, 0, 0, 2, 0), (8, 0, 0, 3, 0), (0, 0, 3),
+    (9, 0, 0, 3, 1), (4, 0, 0, 1, 0), (2, 0, 0, 3, 1), (10, 0, 0, 2), (11, 1), (3, 0, 0, 2, 1),
+    (9, 0, 0, 3, 0), (4, 0, 1, 1, 0), (2, 0, 0, 3, 0), (3, 0, 0, 2, 0), (4, 0, 1, 1, 1),
+    (2, 0, 1, 2, 1), (12, 2), (2, 0, 1, 2, 0), (4, 0, 0, 2, 1), (3, 0, 1, 1, 1), (5, 0, 0, 0),
+    (10, 0, 0, 3), (3, 0, 1, 1, 0), (12, 3), (4, 0, 0, 2, 0), (4, 0, 0, 1, 1), (0, 0, 2), (11, 2),
+    (11, 3), (4, 0, 0, 3, 1), (2, 0, 3, 1, 0), (5, 0, 0, 1), (4, 0, 0, 3, 0), (3, 0, 0, 3, 0),
+    (2, 0, 3, 1, 1), (3, 0, 0, 3, 1), (14, 0, 0, 0), (14, 0, 0, 1), (5, 0, 0, 2), (5, 0, 1, 0),
+    (5, 0, 1, 1), (5, 0, 0, 3), (2, 0, 1, 3, 0), (14, 0, 0, 2), (14, 0, 1, 0), (2, 0, 1, 3, 1),
+    (14, 0, 0, 3), (3, 0, 1, 2, 1), (4, 0, 1, 2, 1), (3, 0, 1, 2, 0), (1, 0, 3), (15, 0, 0, 1),
+    (4, 0, 1, 2, 0), (14, 0, 1, 1), (15, 0, 0, 3), (13,), (5, 0, 1, 2), (4, 0, 1, 3, 0),
+    (4, 0, 1, 3, 1), (4, 0, 3, 1, 1), (16, 0, 0, 3, 1), (1, 0, 2), (16, 0, 0, 3, 0),
+    (15, 0, 0, 2), (2, 0, 2, 1, 1), (3, 0, 1, 3, 0), (2, 0, 2, 1, 0), (14, 0, 1, 2),
+    (2, 0, 3, 2, 1), (16, 0, 0, 2, 1), (3, 0, 1, 3, 1), (2, 0, 3, 2, 0), (16, 0, 0, 2, 0),
+    (15, 0, 1, 1), (3, 0, 3, 1, 1), (5, 0, 3, 0), (5, 0, 1, 3), (3, 0, 3, 1, 0), (17, 0, 0, 3, 0),
+    (17, 0, 0, 3, 1), (14, 0, 1, 3), (17, 0, 0, 2, 1), (3, 0, 2, 1, 1), (17, 0, 0, 2, 0),
+    (15, 0, 1, 3), (16, 0, 0, 1, 0), (5, 0, 2, 0), (14, 0, 3, 0), (16, 0, 1, 3, 1),
+    (2, 0, 2, 2, 1), (16, 0, 0, 1, 1), (2, 0, 3, 3, 0), (4, 0, 2, 1, 0), (4, 0, 3, 1, 0),
+    (3, 0, 3, 2, 0), (15, 0, 1, 2), (2, 0, 3, 3, 1), (2, 0, 2, 2, 0), (4, 0, 2, 1, 1),
+    (16, 0, 1, 3, 0), (16, 0, 1, 2, 1), (3, 0, 2, 1, 0), (16, 0, 1, 2, 0), (17, 0, 1, 3, 1),
+    (4, 0, 3, 2, 1), (5, 0, 3, 1), (17, 0, 1, 3, 0), (4, 0, 3, 3, 0), (3, 0, 3, 2, 1),
+    (17, 0, 0, 1, 0), (17, 0, 0, 1, 1), (4, 0, 3, 2, 0), (15, 0, 0, 0), (14, 0, 3, 1), (18, 0, 0),
+    (5, 0, 2, 1), (17, 0, 1, 2, 1), (4, 0, 3, 3, 1), (2, 0, 2, 3, 1), (5, 0, 3, 2),
+    (16, 0, 1, 1, 1), (3, 0, 2, 2, 0), (17, 0, 1, 2, 0), (3, 0, 2, 2, 1), (15, 0, 1, 0),
+    (14, 0, 3, 2), (16, 0, 1, 1, 0), (3, 0, 3, 3, 0), (14, 0, 2, 0), (2, 0, 2, 3, 0), (19, 0, 0),
+    (20, 0, 0), (3, 0, 3, 3, 1), (0, 1, 0), (5, 0, 3, 3), (14, 0, 3, 3), (3, 0, 2, 3, 1),
+    (15, 0, 3, 1), (17, 0, 1, 1, 1), (4, 0, 2, 2, 0), (17, 0, 1, 1, 0), (18, 0, 1), (1, 1, 0),
+    (15, 0, 3, 3), (5, 1, 0, 0), (4, 0, 2, 2, 1), (2, 1, 0, 1, 0), (16, 0, 3, 3, 0),
+    (2, 1, 0, 1, 1), (16, 0, 3, 3, 1), (3, 0, 2, 3, 0), (19, 0, 1), (4, 0, 2, 3, 1), (20, 0, 1),
+    (5, 0, 2, 2), (4, 0, 2, 3, 0), (0, 1, 1), (14, 0, 2, 1), (15, 0, 3, 2), (17, 0, 3, 3, 1),
+    (4, 1, 0, 1, 0), (17, 0, 3, 3, 0), (3, 1, 0, 1, 1), (14, 0, 2, 2), (5, 0, 2, 3),
+    (16, 0, 3, 2, 1), (2, 1, 0, 2, 1), (16, 0, 3, 2, 0), (3, 1, 0, 1, 0), (2, 1, 0, 2, 0),
+    (14, 0, 2, 3), (2, 1, 1, 1, 1), (2, 1, 1, 1, 0), (1, 1, 1), (15, 0, 2, 3), (16, 0, 2, 3, 0),
+    (16, 0, 3, 1, 1), (16, 0, 3, 1, 0), (16, 0, 2, 3, 1), (2, 1, 0, 3, 0), (3, 1, 0, 2, 1),
+    (15, 0, 3, 0), (5, 1, 1, 0), (4, 1, 0, 2, 0), (15, 0, 2, 2), (2, 1, 0, 3, 1),
+    (17, 0, 3, 2, 1), (4, 1, 0, 1, 1), (17, 0, 3, 2, 0), (2, 1, 1, 2, 1), (17, 0, 2, 3, 1),
+    (3, 1, 0, 2, 0), (4, 1, 0, 3, 0), (3, 1, 1, 1, 0), (4, 1, 0, 2, 1), (14, 1, 0, 0),
+    (17, 0, 2, 3, 0), (14, 1, 1, 0), (16, 0, 2, 2, 1), (5, 1, 0, 1), (2, 1, 1, 2, 0),
+    (4, 1, 1, 1, 1), (14, 1, 0, 1), (15, 0, 2, 1), (18, 0, 3), (3, 1, 1, 1, 1), (15, 0, 2, 0),
+    (5, 1, 0, 2), (16, 0, 2, 2, 0), (3, 1, 0, 3, 1), (17, 0, 3, 1, 0), (4, 1, 0, 3, 1),
+    (14, 1, 0, 2), (17, 0, 3, 1, 1), (3, 1, 0, 3, 0), (17, 0, 2, 2, 1), (17, 0, 2, 2, 0),
+    (5, 1, 0, 3), (16, 0, 2, 1, 0), (3, 1, 1, 2, 0), (3, 1, 1, 2, 1), (16, 0, 2, 1, 1),
+    (4, 1, 1, 1, 0), (2, 1, 1, 3, 1), (2, 1, 1, 3, 0), (14, 1, 0, 3), (19, 0, 3), (20, 0, 3),
+    (0, 1, 3), (3, 1, 1, 3, 1), (4, 1, 1, 3, 0), (17, 0, 2, 1, 1), (17, 0, 2, 1, 0),
+    (4, 1, 1, 3, 1), (5, 1, 1, 1), (18, 0, 2), (3, 1, 1, 3, 0), (4, 1, 1, 2, 0), (4, 1, 1, 2, 1),
+    (15, 1, 0, 3), (14, 1, 1, 1), (1, 1, 3), (5, 1, 1, 3), (16, 1, 0, 3, 1), (2, 1, 3, 1, 0),
+    (5, 1, 1, 2), (16, 1, 0, 3, 0), (14, 1, 1, 2), (2, 1, 3, 1, 1), (14, 1, 1, 3), (19, 0, 2),
+    (20, 0, 2), (0, 1, 2), (15, 1, 1, 3), (16, 1, 1, 3, 1), (16, 1, 1, 3, 0), (15, 1, 0, 2),
+    (3, 1, 3, 1, 0), (17, 1, 0, 3, 0), (15, 1, 1, 2), (4, 1, 3, 1, 0), (16, 1, 0, 2, 1),
+    (3, 1, 3, 1, 1), (17, 1, 0, 3, 1), (17, 1, 1, 3, 1), (4, 1, 3, 1, 1), (2, 1, 3, 2, 0),
+    (5, 1, 3, 0), (2, 1, 3, 2, 1), (17, 1, 1, 3, 0), (1, 1, 2), (16, 1, 1, 2, 1), (5, 1, 3, 1),
+    (14, 1, 3, 0), (16, 1, 0, 2, 0), (2, 1, 2, 1, 0), (16, 1, 1, 2, 0), (14, 1, 3, 1),
+    (2, 1, 2, 1, 1), (2, 1, 3, 3, 0), (17, 1, 1, 2, 0), (2, 1, 3, 3, 1), (15, 1, 1, 1),
+    (3, 1, 3, 2, 0), (17, 1, 1, 2, 1), (3, 1, 3, 2, 1), (4, 1, 3, 3, 1), (17, 1, 0, 2, 0),
+    (15, 1, 0, 1), (16, 1, 1, 1, 0), (4, 1, 3, 2, 1), (16, 1, 0, 1, 0), (4, 1, 3, 2, 0),
+    (4, 1, 3, 3, 0), (16, 1, 1, 1, 1), (3, 1, 3, 3, 0), (3, 1, 3, 3, 1), (2, 1, 2, 2, 1),
+    (17, 1, 0, 2, 1), (16, 1, 0, 1, 1), (5, 1, 3, 2), (2, 1, 2, 2, 0), (14, 1, 3, 2),
+    (5, 1, 3, 3), (17, 1, 1, 1, 1), (15, 1, 1, 0), (17, 1, 1, 1, 0), (15, 1, 0, 0),
+    (3, 1, 2, 1, 1), (4, 1, 2, 1, 1), (14, 1, 3, 3), (18, 1, 1), (15, 1, 3, 3), (16, 1, 3, 3, 0),
+    (16, 1, 3, 3, 1), (17, 1, 0, 1, 1), (2, 1, 2, 3, 1), (3, 1, 2, 1, 0), (18, 1, 0),
+    (17, 1, 0, 1, 0), (19, 1, 1), (20, 1, 1), (15, 1, 3, 2), (16, 1, 3, 2, 1), (17, 1, 3, 3, 1),
+    (3, 1, 2, 2, 0), (5, 1, 2, 0), (15, 1, 3, 1), (17, 1, 3, 3, 0), (3, 1, 2, 2, 1),
+    (2, 1, 2, 3, 0), (16, 1, 3, 2, 0), (4, 1, 2, 1, 0), (21, 1), (14, 1, 2, 0), (4, 1, 2, 2, 0),
+    (0, 2, 1), (5, 1, 2, 1), (4, 1, 2, 2, 1), (19, 1, 0), (20, 1, 0), (14, 1, 2, 1),
+    (16, 1, 3, 1, 1), (17, 1, 3, 2, 0), (15, 1, 3, 0), (4, 1, 2, 3, 1), (16, 1, 3, 1, 0),
+    (3, 1, 2, 3, 0), (4, 1, 2, 3, 0), (17, 1, 3, 2, 1), (5, 1, 2, 2), (3, 1, 2, 3, 1), (21, 0),
+    (0, 2, 0), (14, 1, 2, 2), (5, 1, 2, 3), (14, 1, 2, 3), (2, 2, 1, 1, 0), (2, 2, 1, 1, 1),
+    (17, 1, 3, 1, 0), (17, 1, 3, 1, 1), (15, 1, 2, 3), (16, 1, 2, 3, 1), (2, 2, 0, 1, 1),
+    (1, 2, 1), (17, 1, 2, 3, 1), (2, 2, 0, 1, 0), (15, 1, 2, 2), (18, 1, 3), (16, 1, 2, 3, 0),
+    (17, 1, 2, 3, 0), (15, 1, 2, 1), (5, 2, 1, 0), (16, 1, 2, 2, 1), (2, 2, 1, 2, 1),
+    (15, 1, 2, 0), (16, 1, 2, 2, 0), (4, 2, 1, 1, 1), (1, 2, 0), (2, 2, 1, 2, 0), (19, 1, 3),
+    (2, 2, 0, 2, 1), (17, 1, 2, 2, 1), (5, 2, 0, 0), (17, 1, 2, 2, 0), (3, 2, 1, 1, 1),
+    (2, 2, 1, 3, 1), (3, 2, 1, 1, 0), (4, 2, 1, 1, 0), (2, 2, 0, 2, 0), (20, 1, 3),
+    (4, 2, 0, 1, 1), (16, 1, 2, 1, 0), (3, 2, 0, 1, 1), (16, 1, 2, 1, 1), (3, 2, 0, 1, 0),
+    (17, 1, 2, 1, 0), (17, 1, 2, 1, 1), (14, 2, 1, 0), (21, 3), (0, 2, 3), (2, 2, 0, 3, 0),
+    (4, 2, 0, 1, 0), (18, 1, 2), (14, 2, 0, 0), (3, 2, 0, 2, 1), (4, 2, 1, 2, 0), (3, 2, 0, 2, 0),
+    (2, 2, 0, 3, 1), (4, 2, 0, 2, 0), (3, 2, 1, 2, 1), (5, 2, 0, 1), (19, 1, 2), (4, 2, 0, 3, 0),
+    (1, 2, 3), (20, 1, 2), (2, 2, 3, 1, 1), (3, 2, 0, 3, 0), (3, 2, 1, 2, 0), (2, 2, 3, 1, 0),
+    (21, 2), (3, 2, 3, 1, 1), (4, 2, 0, 2, 1), (4, 2, 1, 3, 1), (0, 2, 2), (5, 2, 1, 1),
+    (14, 2, 1, 1), (2, 2, 3, 2, 1), (5, 2, 0, 2), (14, 2, 0, 1), (3, 2, 3, 1, 0), (2, 2, 1, 3, 0),
+    (3, 2, 1, 3, 1), (3, 2, 0, 3, 1), (4, 2, 1, 2, 1), (2, 2, 3, 2, 0), (4, 2, 3, 1, 1),
+    (4, 2, 0, 3, 1), (5, 2, 3, 0), (2, 2, 2, 1, 1), (14, 2, 0, 2), (2, 2, 2, 1, 0),
+    (4, 2, 3, 1, 0), (5, 2, 0, 3), (2, 2, 3, 3, 0), (1, 2, 2), (3, 2, 1, 3, 0), (14, 2, 3, 0),
+    (5, 2, 3, 1), (4, 2, 1, 3, 0), (14, 2, 3, 1), (2, 2, 2, 2, 0), (2, 2, 3, 3, 1), (5, 2, 1, 3),
+    (4, 2, 3, 2, 1), (5, 2, 1, 2), (3, 2, 3, 2, 0), (2, 2, 2, 2, 1), (14, 2, 0, 3),
+    (2, 2, 2, 3, 1), (14, 2, 1, 2), (5, 2, 2, 0), (4, 2, 3, 3, 1), (3, 2, 2, 1, 1),
+    (4, 2, 3, 2, 0), (3, 2, 2, 1, 0), (4, 2, 2, 1, 0), (4, 2, 2, 1, 1), (3, 2, 3, 2, 1),
+    (4, 2, 3, 3, 0), (2, 2, 2, 3, 0), (14, 2, 2, 0), (14, 2, 1, 3), (3, 2, 3, 3, 0),
+    (3, 2, 3, 3, 1), (5, 2, 2, 1), (5, 2, 3, 2), (3, 2, 2, 2, 1), (3, 2, 2, 2, 0), (14, 2, 2, 1),
+    (14, 2, 3, 2), (5, 2, 3, 3), (4, 2, 2, 2, 0), (3, 2, 2, 3, 0), (4, 2, 2, 2, 1),
+    (4, 2, 2, 3, 0), (4, 2, 2, 3, 1), (3, 2, 2, 3, 1), (14, 2, 3, 3), (5, 2, 2, 2), (5, 2, 2, 3),
+    (14, 2, 2, 2), (14, 2, 2, 3),
+)
+ROUTE = ("S", "H0", "H", "K", "O", "R")
+CHAINS = 1 + max(step[2] for step in ORDER if NAMES[step[0]] == "aS")
+PLANES = 1 + max(step[3] for step in ORDER if NAMES[step[0]] == "U")
+GATHER_SPLIT = ((13, 11, 10, 10), (9, 9, 9, 9), (10, 10, 11, 13))
+SCATTER_SPLIT = ((10, 10, 10, 10), (10, 10, 10, 10))
+
+
+class Plan:
+    def __init__(self, experts, groups, rows, width, hidden, slots):
+        self.experts, self.groups, self.rows, self.width = experts, groups, rows, width
+        self.hidden, self.slots = hidden, slots
+        self.capacity = slots // experts
+        self.planes = experts // 4
+        self.chains = CHAINS
+        self.n = rows // self.chains
+        self.gather_split = [[self.cut(c) for c in line] for line in GATHER_SPLIT]
+        self.scatter_split = [[self.cut(c) for c in line] for line in SCATTER_SPLIT]
+        self.lent = max(max(line) for line in self.scatter_split)
+        self.rest = width - min(min(line) for line in self.scatter_split)
+
+    def cut(self, sixteenths):
+        return self.width * sixteenths // 16
+
+    def fits(self):
+        lanes = 128
+        whole = (
+            self.groups == 2
+            and self.experts % 4 == 0
+            and 2 * self.experts <= lanes
+            and self.planes == PLANES
+            and self.rows == lanes
+            and self.n % 16 == 0
+            and self.width % 2048 == 0
+            and self.hidden % (2 * lanes) == 0
+            and (2 * self.capacity) % 16 == 0
+            and 2 * self.capacity <= 2 * lanes
+            and max(self.slots, self.width) <= self.rows * self.experts
+            and 2 * self.hidden <= self.width
+        )
+        return whole and self.bytes() <= 63 * 1024 * 1024
+
+    def bytes(self):
+        e, r, d, h, z = self.experts, self.rows, self.width, self.hidden, self.planes
+        tokens = 2 * e * r * d * 2 + e * r * d * 2 + e * r * d
+        lines = self.chains * self.n * (2 * z * (d + self.rest) + z * self.lent + self.rest) * 2
+        return tokens + lines + 2 * d * h * 2 + e * r * h * (4 + 2 + 2) + 3 * r * d * 2 + d * h * 2 + d * h
+
+    def semaphores(self):
+        chain = ("rail", "rail2", "over", "sib", "gift", "lend", "sum", "sum2", "last", "swap")
+        whole = sum(semaphores_of(self.planes, (kind,)) for kind in chain) * self.chains
+        table = sum(semaphores_of(self.planes, (kind,)) for kind in ("rail", "over", "sib"))
+        return whole + table + 1
+
+
+def semaphores_of(planes, kind):
+    sizes = {"rail": planes + 1, "rail2": planes + 1, "sum": planes + 1, "sum2": planes + 1}
+    sizes.update(over=planes, sib=planes, gift=planes, lend=planes)
+    return sizes.get(kind[0], 1)
+
+
+def fused_kernel(
+    plan,
+    cot,
+    ids,
+    gates,
+    hidden_hbm,
+    up_hbm,
+    down_hbm,
+    grad_in_hbm,
+    grad_w_hbm,
+    grad_in,
+    grad_w,
+    view,
+    part,
+    gift,
+    came,
+    came2,
+    rung,
+    last,
+    slope,
+    act,
+    first,
+    third,
+    tabs,
+    own_tab,
+    turn,
+    scaled,
+    up,
+    down,
+    total,
+    send_sems,
+    recv_sems,
+    load_sems,
+):
+    experts, planes, chains, n = plan.experts, plan.planes, plan.chains, plan.n
+    width, hidden, cap = plan.width, plan.hidden, plan.capacity
+    top = ids.shape[0]
+    span = experts * n
+    half = width // 2
+    me = lax.axis_index("expert")
+    token = lax.axis_index("token")
+    core = me % 2
+    y = (me // 2) % 2
+    z = me // 4
+    has = {0: z > 0, 1: z < planes - 1}
+    up_peer = {"expert": me + 4}
+    down_peer = {"expert": me - 4}
+    rung_peer = {"expert": me + 2 - 4 * y}
+    sib_peer = {"expert": me + 1 - 2 * core}
+    far_peer = {"token": 1 - token}
+    sources = ((0, up_peer), (1, down_peer))
+    full = pl.ds(0, width)
+
+    def sides(split):
+        return pl.ds(0, split), pl.ds(split, width - split)
+
+
+    bases = {}
+
+    def number(key):
+        kind, at = key
+        if kind not in bases:
+            bases[kind] = sum(semaphores_of(planes, name) for name in bases)
+        return bases[kind] + at
+
+    def copy(key, src, dst, peer):
+        at = number(key)
+        return pltpu.make_async_remote_copy(
+            src_ref=src,
+            dst_ref=dst,
+            send_sem=send_sems.at[at],
+            recv_sem=recv_sems.at[at],
+            device_id=peer,
+            device_id_type=MESH,
+        )
+
+    def when(cond, action):
+        if cond is None:
+            action()
+        else:
+            pl.when(cond)(action)
+
+    pending = {}
+
+    def post(group, cond, key, src, dst, peer):
+        when(cond, lambda: copy(key, src, dst, peer).start())
+        if group is not None:
+            owe(group, cond, key, src)
+
+    def owe(group, cond, key, src):
+        pending.setdefault(group, []).append((cond, key, src))
+
+    def drain(group):
+        for cond, key, src in pending.pop(group, []):
+            when(cond, lambda: copy(key, src, src, sib_peer).wait_send())
+
+    def arrive(cond, key, dst):
+        when(cond, lambda: copy(key, dst, dst, sib_peer).wait_recv())
+
+    def both(a, b):
+        return b if a is None else (a if b is None else jnp.logical_and(a, b))
+
+    def slot_of(p, yy, cc):
+        return 4 * p + 2 * cc + yy
+
+    def origin(way, d):
+        return z - d if way == 0 else z + d
+
+    def there(way, d):
+        return z >= d if way == 0 else z + d < planes
+
+    mine = slot_of(z, y, core)
+    beside = slot_of(z, 1 - y, core)
+
+    def gather(tag, at, src, split):
+        group = ("ag", tag)
+        whole = split is None
+        c1, c2 = sides(width if whole else split)
+        rail = lambda way, p: (("rail", tag), p + way)
+        rail2 = lambda way, p: (("rail2", tag), p + way)
+        across_key = lambda p: (("over", tag), p)
+        sib = lambda p: (("sib", tag), p)
+
+        def pair(p, cc):
+            return at(slot_of(p, 0, cc), full, 2)
+
+        def start():
+            drain(group)
+            post(group, None, across_key(z), src, at(mine, full), rung_peer)
+            for way, peer in sources:
+                post(group, has[1 - way], rail(way, z), src, at(mine, full), peer)
+            post(None, None, sib(z), src, at(mine, full), sib_peer)
+            owe(group, None, sib(z), pair(z, core))
+
+        def meet():
+            block = at(beside, full)
+            arrive(None, across_key(z), block)
+            if not whole:
+                cut = at(beside, c2)
+                for way, peer in sources:
+                    post(group, has[1 - way], rail2(way, z), cut, cut, peer)
+            post(None, None, sib(z), block, block, sib_peer)
+
+        def hop(d, way):
+            peer = sources[way][1]
+            cond = there(way, d)
+            p = origin(way, d)
+            block = at(slot_of(p, y, core), full)
+            arrive(cond, rail(way, p), block)
+            if d + 1 < planes:
+                post(group, both(cond, has[1 - way]), rail(way, p), block, block, peer)
+            cut = block if whole else at(slot_of(p, y, core), c1)
+            post(group, cond, across_key(p), cut, cut, rung_peer)
+            post(None, cond, sib(p), block, block, sib_peer)
+            owe(group, cond, sib(p), pair(p, core))
+
+        def hop2(d, way):
+            peer = sources[way][1]
+            cond = there(way, d)
+            p = origin(way, d)
+            cut = at(slot_of(p, 1 - y, core), c2)
+            arrive(cond, rail2(way, p), cut)
+            if d + 1 < planes:
+                post(group, both(cond, has[1 - way]), rail2(way, p), cut, cut, peer)
+            post(None, cond, sib(p), cut, cut, sib_peer)
+
+        def across(d, way):
+            cond = there(way, d)
+            p = origin(way, d)
+            cut = at(slot_of(p, 1 - y, core), full if whole else c1)
+            arrive(cond, across_key(p), cut)
+            post(None, cond, sib(p), cut, cut, sib_peer)
+
+        def ready(d):
+            if d == 0:
+                arrive(None, sib(z), pair(z, 1 - core))
+                return
+            for way in range(2):
+                p = origin(way, d)
+                arrive(there(way, d), sib(p), pair(p, 1 - core))
+
+        return start, meet, hop, hop2, across, ready
+
+    def plane_at(i):
+        low = jnp.minimum(z, planes - 1 - z)
+        near = jnp.where(z < planes // 2, 1, -1)
+        d = jnp.where(i <= 2 * low, (i + 1) // 2, i - low)
+        pair = jnp.where(z % 2 == 0, 1, -1)
+        sign = jnp.where(i <= 2 * low, pair * (1 if i % 2 else -1), near)
+        return z + sign * d if i else z
+
+    tab_at = lambda slot, cols, count=0: tabs.at[pl.ds(slot, count) if count else slot]
+
+    sources_of = {0: cot, 1: first, 2: third}
+
+    def chain_rows(chain):
+        return pl.ds(chain * n, n)
+
+    stages = {}
+    for chain in range(chains):
+        for f in range(3):
+
+            def at(slot, cols, count=1, f=f, chain=chain):
+                rows = pl.ds(pl.multiple_of(chain * span + slot * n, n), count * n)
+                return view.at[f % 2, rows, cols]
+
+            src = sources_of[f].at[chain_rows(chain)]
+            stages[f, chain] = gather(chain, at, src, plan.gather_split[f][chain])
+
+    def start(f, chain):
+        stages[f, chain][0]()
+        rows = pl.ds(pl.multiple_of(chain * span + mine * n, n), n)
+        view[f % 2, rows, :] = sources_of[f][chain_rows(chain), :]
+
+    hidden_at = view.at[1, pl.ds(0, plan.slots), pl.ds(0, hidden)]
+    up_at = view.at[1, pl.ds(0, width), pl.ds(hidden, hidden)]
+    loads = [
+        pltpu.make_async_copy(hidden_hbm, hidden_at, load_sems.at[0]),
+        pltpu.make_async_copy(up_hbm, up_at, load_sems.at[1]),
+        pltpu.make_async_copy(down_hbm, down, load_sems.at[2]),
+    ]
+    turns = 4
+
+    def turn_up(k):
+        size = width // turns
+        if k == 0:
+            loads[1].wait()
+        up[:, k * size : (k + 1) * size] = view[
+            1, k * size : (k + 1) * size, hidden : 2 * hidden
+        ].T
+        if k == turns - 1:
+            loads[2].wait()
+
+    def make_table():
+        lanes = plan.rows
+        kind = lax.broadcasted_iota(jnp.int32, (2 * experts, lanes), 0)
+        lane = lax.broadcasted_iota(jnp.int32, (lanes, lanes), 1)
+        row = lax.broadcasted_iota(jnp.int32, (lanes, lanes), 0)
+        match = jnp.zeros(kind.shape, jnp.float32)
+        gate = jnp.zeros(kind.shape, jnp.float32)
+        for k in range(top):
+            name = ids[k : k + 1, :]
+            match = match + jnp.where(name == kind, 1.0, 0.0)
+            gate = gate + jnp.where(name + experts == kind, gates[k : k + 1, :], 0.0)
+        before = jnp.where(row < lane, 1.0, 0.0).astype(jnp.bfloat16)
+        rank = jnp.dot(match.astype(jnp.bfloat16), before, preferred_element_type=jnp.float32)
+        rank = jnp.where(match > 0.5, rank, -4.0 * lanes)
+        table = jnp.where(kind < experts, rank, gate)
+        own_tab[...] = table
+        tabs[mine] = table
+
+    tile = 256
+
+    def prepare(i):
+        p = plane_at(i)
+        if i == 0:
+            loads[0].wait()
+            turn[...] = jnp.zeros_like(turn)
+        for j in range(4):
+            turn[pl.ds(j, 1), :] = tabs[4 * p + j, pl.ds(me, 1), :]
+            turn[pl.ds(4 + j, 1), :] = tabs[4 * p + j, pl.ds(experts + me, 1), :]
+        turned = turn[...].T
+        spot = lax.broadcasted_iota(jnp.int32, (plan.rows, 2 * cap), 1).astype(jnp.float32)
+
+        @pl.loop(0, hidden // tile)
+        def _(step):
+            cols = pl.ds(pl.multiple_of(step * tile, tile), tile)
+            for yy in range(2):
+                rows = pl.ds(pl.multiple_of((4 * p + 2 * yy) * cap, 2 * cap), 2 * cap)
+                values = view[1, rows, cols].astype(jnp.float32)
+                normal_cdf = 0.5 * (1.0 + lax.erf(values * root_half))
+                density = inv_root_two_pi * jnp.exp(-0.5 * values * values)
+                steep = normal_cdf + values * density
+                active = (values * normal_cdf).astype(jnp.bfloat16)
+                high = steep.astype(jnp.bfloat16)
+                low = (steep - high.astype(jnp.float32)).astype(jnp.bfloat16)
+                for cc in range(2):
+                    j = 2 * cc + yy
+                    sel = jnp.where(turned[:, j : j + 1] + float(cc * cap) == spot, 1.0, 0.0)
+                    sel = sel.astype(jnp.bfloat16)
+                    gate = turned[:, 4 + j : 5 + j]
+                    pick = lambda rhs: jnp.dot(sel, rhs, preferred_element_type=jnp.float32)
+                    steeps = (pick(high) + pick(low)) * gate
+                    actives = (pick(active) * gate).astype(jnp.bfloat16)
+                    for chain in range(chains):
+                        cut = slice(chain * n, (chain + 1) * n)
+                        to = pl.multiple_of(chain * span + (4 * p + j) * n, n)
+                        slope[pl.ds(to, n), cols] = steeps[cut]
+                        act[chain, p, 0, j * n : (j + 1) * n, cols] = actives[cut]
+
+        if i == planes - 1:
+            post("act", None, (("act",), 0), act.at[:, :, 0], act.at[:, :, 1], far_peer)
+
+    unit_rows = 8 * n
+
+    def pair_at(i):
+        mine_first = z // 2 * 2
+        return mine_first if i == 1 else planes - 2 - mine_first
+
+    def apply(f, chain, i):
+        if i % 2 == 0:
+            return
+        base = pl.multiple_of(chain * span + pair_at(i) * 4 * n, unit_rows)
+        rows = pl.ds(base, unit_rows)
+        if i == 1:
+            drain(("rs", chain))
+        inner = jnp.dot(view[f % 2, rows, :], down[...], preferred_element_type=jnp.float32)
+        scaled[...] = (inner * slope[rows, :]).astype(jnp.bfloat16)
+        wide = width // 2
+
+        @pl.loop(0, width // wide)
+        def _(step):
+            cols = pl.ds(pl.multiple_of(step * wide, wide), wide)
+            piece = jnp.dot(scaled[...], up[:, cols], preferred_element_type=jnp.float32)
+            part[rows, cols] = piece.astype(jnp.bfloat16)
+
+        for k in (i - 1, i):
+            p = plane_at(k)
+            away = pl.multiple_of(chain * span + p * 4 * n + (1 - core) * 2 * n, 2 * n)
+            post(
+                ("rs", chain),
+                None,
+                (("gift", chain), p),
+                part.at[pl.ds(away, 2 * n)],
+                gift.at[chain, p],
+                sib_peer,
+            )
+
+    def part_rows(chain, p, yy):
+        return pl.ds(pl.multiple_of(chain * span + slot_of(p, yy, core) * n, n), n)
+
+    patch = 128
+
+    def add_up(cols, terms, store):
+        @pl.loop(0, cols.size // patch)
+        def _(step):
+            offset = pl.multiple_of(step * patch, patch)
+            value = None
+            for term, shift in terms:
+                x = term(pl.ds(pl.multiple_of(offset + shift, patch), patch)).astype(jnp.float32)
+                value = x if value is None else value + x
+            store(pl.ds(pl.multiple_of(offset + cols.start, patch), patch), value)
+
+    def from_part(chain, p, yy, cols):
+        return (lambda at: part[part_rows(chain, p, yy), at]), cols.start
+
+    def to_part(chain, p, yy):
+        def store(at, value):
+            part[part_rows(chain, p, yy), at] = value.astype(jnp.bfloat16)
+
+        return store
+
+    def from_gift(chain, p, yy, cols):
+        rows = pl.ds(pl.multiple_of(yy * n, n), n)
+        return (lambda at: gift[chain, p, rows, at]), cols.start
+
+    def from_came(chain, way, p, cols):
+        return (lambda at: came[chain, way, p, :, at]), cols.start
+
+    def from_came2(chain, way, p):
+        return (lambda at: came2[chain, way, p, :, at]), 0
+
+    def lend(f, chain, i):
+        p = plane_at(i)
+        c1 = pl.ds(0, plan.scatter_split[f][chain])
+        arrive(None, (("gift", chain), p), gift.at[chain, p])
+        add_up(
+            full,
+            [from_part(chain, p, 1 - y, full), from_gift(chain, p, 1 - y, full)],
+            to_part(chain, p, 1 - y),
+        )
+        src = part.at[part_rows(chain, p, 1 - y), c1]
+        post(("rs", chain), None, (("lend", chain), p), src, rung.at[chain, p, :, c1], rung_peer)
+
+    def lent(chain, p, c1):
+        arrive(None, (("lend", chain), p), rung.at[chain, p, :, c1])
+
+    def carry2(f, chain, d, way):
+        c2 = sides(plan.scatter_split[f][chain])[1]
+        place = came2.at[chain, way, :, :, pl.ds(0, c2.size)]
+        peer = sources[way][1]
+        to = z + d if way == 0 else z - d
+        cond = there(1 - way, d)
+        src = part.at[part_rows(chain, to, 1 - y), c2]
+
+        @pl.when(cond)
+        def _():
+            if d + 1 < planes:
+                arrive(has[way], (("sum2", chain), to + 1 - way), place.at[to])
+            add_up(
+                c2,
+                [from_part(chain, to, 1 - y, c2), from_came2(chain, way, to)],
+                to_part(chain, to, 1 - y),
+            )
+            copy((("sum2", chain), to + 1 - way), src, place.at[to], peer).start()
+
+        owe(("rs", chain), cond, (("sum2", chain), to + 1 - way), src)
+
+    def carry1(f, chain, d, way):
+        c1, c2 = sides(plan.scatter_split[f][chain])
+        peer = sources[way][1]
+        to = z + d if way == 0 else z - d
+        cond = there(1 - way, d)
+        src = part.at[part_rows(chain, to, y)]
+
+        @pl.when(cond)
+        def _():
+            lent(chain, to, c1)
+            if d + 1 < planes:
+                arrive(has[way], (("sum", chain), to + 1 - way), came.at[chain, way, to])
+            for cols in (c1, c2):
+                terms = [
+                    from_part(chain, to, y, cols),
+                    from_gift(chain, to, y, cols),
+                    from_came(chain, way, to, cols),
+                ]
+                if cols is c1:
+                    terms.append(((lambda at: rung[chain, to, :, at]), 0))
+                add_up(cols, terms, to_part(chain, to, y))
+            copy((("sum", chain), to + 1 - way), src, came.at[chain, way, to], peer).start()
+
+        owe(("rs", chain), cond, (("sum", chain), to + 1 - way), src)
+
+    def settle2(f, chain):
+        c2 = sides(plan.scatter_split[f][chain])[1]
+        short = pl.ds(0, c2.size)
+        for way in range(2):
+            arrive(has[way], (("sum2", chain), z + 1 - way), came2.at[chain, way, z, :, short])
+        add_up(
+            c2,
+            [from_part(chain, z, 1 - y, c2)] + [from_came2(chain, w, z) for w in range(2)],
+            to_part(chain, z, 1 - y),
+        )
+        src = part.at[part_rows(chain, z, 1 - y), c2]
+        post(("rs", chain), None, (("last", chain), 0), src, last.at[chain, :, short], rung_peer)
+
+    def finish(f, chain, cols, extra):
+        rows = chain_rows(chain)
+
+        def store(at, value):
+            term = value.astype(jnp.bfloat16)
+            if f == 0:
+                first[rows, at] = term
+            else:
+                whole = (
+                    cot[rows, at].astype(jnp.float32)
+                    + first[rows, at].astype(jnp.float32)
+                    + term.astype(jnp.float32)
+                )
+                grad_in[rows, at] = whole.astype(jnp.bfloat16)
+
+        terms = [from_part(chain, z, y, cols), from_gift(chain, z, y, cols), extra]
+        add_up(cols, terms + [from_came(chain, w, z, cols) for w in range(2)], store)
+
+    def settle1(f, chain):
+        c1 = pl.ds(0, plan.scatter_split[f][chain])
+        lent(chain, z, c1)
+        for way in range(2):
+            arrive(has[way], (("sum", chain), z + 1 - way), came.at[chain, way, z])
+        finish(f, chain, c1, ((lambda at: rung[chain, z, :, at]), 0))
+
+    def settle(f, chain):
+        c2 = sides(plan.scatter_split[f][chain])[1]
+        arrive(None, (("last", chain), 0), last.at[chain, :, pl.ds(0, c2.size)])
+        finish(f, chain, c2, ((lambda at: last[chain, :, at]), 0))
+        if f == 1:
+            swap(chain)
+            rows = chain_rows(chain)
+            save(chain, grad_in.at[rows], grad_in_hbm.at[rows])
+
+    saved = []
+
+    def save(at, src, dst):
+        copy_out = pltpu.make_async_copy(src, dst, load_sems.at[at])
+        copy_out.start()
+        saved.append(copy_out)
+
+    def swap(chain):
+        rows = chain_rows(chain)
+        away = pl.ds(pl.multiple_of((1 - token) * half, half), half)
+        keep = pl.ds(pl.multiple_of(token * half, half), half)
+        post(
+            "swap",
+            None,
+            (("swap", chain), 0),
+            grad_in.at[rows, away],
+            third.at[rows, pl.ds(half, half)],
+            far_peer,
+        )
+        third[rows, pl.ds(0, half)] = grad_in[rows, keep]
+
+    def swapped(chain):
+        arrive(None, (("swap", chain), 0), third.at[chain_rows(chain), pl.ds(half, half)])
+
+    def weigh(chain, i, end):
+        if i % 2 == 0:
+            return
+        p = pair_at(i)
+        start = pl.multiple_of(chain * span + p * 4 * n, unit_rows)
+        upper = pl.ds(start, 4 * n)
+        lower = pl.ds(pl.multiple_of(start + 4 * n, 4 * n), 4 * n)
+
+        @pl.loop(0, half // tile)
+        def _(step):
+            base = pl.multiple_of(step * tile, tile)
+            out = pl.ds(base, tile)
+            left = pl.ds(base, tile)
+            right = pl.ds(pl.multiple_of(half + base, tile), tile)
+            value = lax.dot_general(
+                jnp.concatenate(
+                    [view[0, rows, cols] for rows in (upper, lower) for cols in (left, right)],
+                    axis=0,
+                ),
+                act[chain, pl.ds(p, 2)].reshape(2 * unit_rows, hidden),
+                (((0,), (0,)), ((), ())),
+                preferred_element_type=jnp.float32,
+            )
+            if end:
+                grad_w[out, :] = ((total[out, :] + value) * grad_scale).astype(jnp.bfloat16)
+                pltpu.make_async_copy(
+                    grad_w.at[out], grad_w_hbm.at[out], load_sems.at[chains + step]
+                ).start()
+            else:
+                total[out, :] += value
+
+        if end:
+            for step in range(half // tile):
+                out = pl.ds(step * tile, tile)
+                saved.append(
+                    pltpu.make_async_copy(
+                        grad_w.at[out], grad_w_hbm.at[out], load_sems.at[chains + step]
+                    )
+                )
+
+    for load in loads:
+        load.start()
+    barrier = pltpu.get_barrier_semaphore()
+    for cond, peer in (
+        (has[1], up_peer),
+        (has[0], down_peer),
+        (None, rung_peer),
+        (None, sib_peer),
+        (None, far_peer),
+    ):
+        when(
+            cond,
+            lambda: pl.semaphore_signal(barrier, inc=1, device_id=peer, device_id_type=MESH),
+        )
+    make_table()
+    count = 3 + jnp.where(z > 0, 1, 0) + jnp.where(z < planes - 1, 1, 0)
+    pl.semaphore_wait(barrier, count)
+
+    def clear():
+        total[...] = jnp.zeros_like(total)
+        for way in range(2):
+
+            @pl.when(jnp.logical_not(has[way]))
+            def _():
+                for chain in range(chains):
+                    came[chain, way] = jnp.zeros(came.shape[2:], came.dtype)
+                    came2[chain, way] = jnp.zeros(came2.shape[2:], came2.dtype)
+
+    units = [0]
+
+    def unit(f, chain, i):
+        if f < 2:
+            apply(f, chain, i)
+            return
+        if units[0] == 0:
+            arrive(None, (("act",), 0), act.at[:, :, 1])
+        units[0] += 1
+        weigh(chain, i, units[0] == chains * planes)
+
+    tab = gather("tab", tab_at, own_tab, None)
+    routes = {("a", f, c): stages[f, c] for f in range(3) for c in range(chains)}
+    routes["t", 0, 0] = tab
+    actions = {
+        "P": prepare,
+        "X": turn_up,
+        "N": clear,
+        "U": unit,
+        "L": lend,
+        "D": carry2,
+        "C": carry1,
+        "T2": settle2,
+        "T1": settle1,
+        "T": settle,
+        "W": swapped,
+        "aS": start,
+        "tS": lambda f, c: tab[0](),
+    }
+    for kind, *args in ORDER:
+        name = NAMES[kind]
+        with jax.named_scope("_".join([name] + [str(a) for a in args])):
+            if name in actions:
+                actions[name](*args)
+            else:
+                routes[(name[0],) + tuple(args[:2])][ROUTE.index(name[1:])](*args[2:])
+    for group in list(pending):
+        drain(group)
+    for copy_out in saved:
+        copy_out.wait()
+
+
+def fused(plan, cotangent, expert_ids, gate_values, hidden_pre, up_weight, down_weight):
+    experts, planes, chains, n = plan.experts, plan.planes, plan.chains, plan.n
+    width, hidden, rows = plan.width, plan.hidden, plan.rows
+    half = width // 2
+    low, dma = jnp.bfloat16, pltpu.SemaphoreType.DMA
+    vmem = pl.BlockSpec(memory_space=pltpu.VMEM)
+    hbm = pl.BlockSpec(memory_space=pl.ANY)
+    count = plan.semaphores()
+    return pl.pallas_call(
+        functools.partial(fused_kernel, plan),
+        out_shape=[
+            jax.ShapeDtypeStruct((rows, width), low),
+            jax.ShapeDtypeStruct((half, hidden), low),
+        ],
+        in_specs=[vmem, vmem, vmem, hbm, hbm, hbm],
+        out_specs=[hbm, hbm],
+        scratch_shapes=[
+            pltpu.VMEM((rows, width), low),
+            pltpu.VMEM((half, hidden), low),
+            pltpu.VMEM((2, chains * experts * n, width), low),
+            pltpu.VMEM((chains * experts * n, width), low),
+            pltpu.VMEM((chains, planes, 2 * n, width), low),
+            pltpu.VMEM((chains, 2, planes, n, width), low),
+            pltpu.VMEM((chains, 2, planes, n, plan.rest), low),
+            pltpu.VMEM((chains, planes, n, plan.lent), low),
+            pltpu.VMEM((chains, n, plan.rest), low),
+            pltpu.VMEM((chains * experts * n, hidden), jnp.float32),
+            pltpu.VMEM((chains, planes, 2, 4 * n, hidden), low),
+            pltpu.VMEM((rows, width), low),
+            pltpu.VMEM((rows, width), low),
+            pltpu.VMEM((experts, 2 * experts, rows), jnp.float32),
+            pltpu.VMEM((2 * experts, rows), jnp.float32),
+            pltpu.VMEM((rows, rows), jnp.float32),
+            pltpu.VMEM((8 * n, hidden), low),
+            pltpu.VMEM((hidden, width), low),
+            pltpu.VMEM((width, hidden), low),
+            pltpu.VMEM((half, hidden), jnp.float32),
+            dma((count,)),
+            dma((count,)),
+            dma((max(3, chains + half // 256),)),
+        ],
+        compiler_params=pltpu.CompilerParams(
+            collective_id=5, has_side_effects=True, vmem_limit_bytes=67_043_328
+        ),
+        cost_estimate=pl.CostEstimate(
+            flops=40_000_000_000, bytes_accessed=20_000_000, transcendentals=0
+        ),
+        name="fused",
+    )(cotangent, expert_ids.T, gate_values.T, hidden_pre, up_weight, down_weight)
+
+
+def hand_on_kernel(count, pieces, *refs):
+    sources, targets, held = refs[:count], refs[count : 2 * count], refs[2 * count : 3 * count]
+    into, out = refs[3 * count :]
+    loads, stores = [], []
+    for i in range(count):
+        size = sources[i].shape[0] // pieces
+        for k in range(pieces):
+            rows = pl.ds(k * size, size)
+            at = i * pieces + k
+            loads.append(
+                pltpu.make_async_copy(sources[i].at[rows], held[i].at[rows], into.at[at])
+            )
+            stores.append(
+                pltpu.make_async_copy(held[i].at[rows], targets[i].at[rows], out.at[at])
+            )
+    for load in loads:
+        load.start()
+    for load, store in zip(loads, stores):
+        load.wait()
+        store.start()
+    for store in stores:
+        store.wait()
+
+
+def hand_on(arrays):
+    count, pieces = len(arrays), 4
+    place = pl.BlockSpec(memory_space=pl.ANY)
+    dma = pltpu.SemaphoreType.DMA
+    return pl.pallas_call(
+        functools.partial(hand_on_kernel, count, pieces),
+        out_shape=[jax.ShapeDtypeStruct(a.shape, a.dtype) for a in arrays],
+        in_specs=[place] * count,
+        out_specs=[place] * count,
+        scratch_shapes=[pltpu.VMEM(a.shape, a.dtype) for a in arrays]
+        + [dma((count * pieces,)), dma((count * pieces,))],
+        name="hand_on",
+    )(*arrays)
+
+
+def body(cotangent, expert_ids, gate_values, hidden_pre, up_weight, down_weight):
+    plan = Plan(
+        lax.axis_size("expert"),
+        lax.axis_size("token"),
+        cotangent.shape[0],
+        cotangent.shape[1],
+        hidden_pre.shape[2],
+        hidden_pre.shape[1],
+    )
+    if not plan.fits():
+        return staged(cotangent, expert_ids, gate_values, hidden_pre, up_weight, down_weight)
+    input_grad, grad_out = fused(
+        plan, cotangent, expert_ids, gate_values, hidden_pre[0], up_weight[0], down_weight[0]
+    )
+    input_grad, grad_out = hand_on([input_grad, grad_out])
+    return (input_grad, grad_out[None])
+
+
 def solution(mesh):
     in_specs = (
         P(("expert", "token"), None),

time: 302 us -> 195 us (0.65)
  matrix products: 45.9 us -> 0 us
  Pallas kernels: 233 us -> 194 us
  other arithmetic: 7.33 us -> 0 us
  waiting for transfers between devices: 5.3 us -> 0 us
  starting transfers between devices: 4.55 us -> 0 us
  local copies, waits for them, and re-layouts: 4.46 us -> 0 us
    dot_general x9 -> x0, matrix products: 45.9 us -> none  [the longest x2 22 us: transpose_jacobian(): lax.dot_general(scaled, up_weight, (((1,), (1,)), ((), ())), preferred_el...]
    pallas_call x5 -> x2, Pallas kernels: 233 us -> 194 us  [the longest x1 191 us: fused(): pl.pallas_call(functools.partial(fused_kernel, plan), out_shape=[jax.Shap...]
    ppermute x3 -> x0, waiting for transfers between devices: 5.3 us -> none  [from_groups(): taken.append(lax.ppermute(make((mine + shift) % groups), 'token', pairs))]
    ppermute x3 -> x0, starting transfers between devices: 4.55 us -> none  [from_groups(): taken.append(lax.ppermute(make((mine + shift) % groups), 'token', pairs))]
    convert_element_type x4 -> x0, other arithmetic: 4.35 us -> none  [the longest x2 3.27 us: slope_and_act(): active = (values * normal_cdf).astype(jnp.bfloat16)]
    unnamed x19 -> x0, local copies, waits for them, and re-layouts: 4.3 us -> none
  transfers between devices with their start and end apart: 3 -> 0, of which waited for: 1 -> 0; matrix products, arithmetic and copies ran while one was open for 15% -> 0% of each run, Pallas kernels for 77% -> 0%
where the time goes in v2:
time: 195 us
  Pallas kernels  194 us (99%)
    pallas_call x1, Pallas kernels, fused(): pl.pallas_call(functools.partial(fused_kernel, plan), out_shape=[jax.Shap...  191 us

profile of v2, /device:TPU:0, one launch (start us, length us, event | category | flops | bytes accessed | tf_op | source)
XLA Modules:
  0.0 194.5 jit_solution(11199110278190190477)
XLA Ops:
  0.6 191.2 %fused.1 = (bf16[128,2048]{1,0:T(8,128)(2,1)}, bf16[1024,768]{1,0:T(8,128)(2,1)}) custom-call(bf16[128,2048]{1,0:T(8,128)(2,1)} %cot.1, s32[6,128]{1,0:T(8,128)} %bitcast.10, f32[6,128]{1,0:T(8,128)} %bitcast.11, bf16[896,768]{1,0:T(8,128)(2,1)} %bitcast.9, bf16[2048,768]{1,0:T(8,128)(2,1)} %bitcast.6, bf16[2048,768]{1,0:T(8,128)(2,1)} %bitcast.7), custom_call_target="tpu_custom_call" | custom-call | flops 40000000000 | bytes 20000000 | tf_op jit(solution)/shard_map/fused/pallas_call | solution.py:1176
  191.8 2.5 %hand_on.1 = (bf16[128,2048]{1,0:T(8,128)(2,1)}, bf16[1024,768]{1,0:T(8,128)(2,1)}) custom-call(bf16[128,2048]{1,0:T(8,128)(2,1)} %get-tuple-element.6.refs_0_, bf16[1024,768]{1,0:T(8,128)(2,1)} %get-tuple-element.7.refs_1_), custom_call_target="tpu_custom_call" | custom-call | tf_op jit(solution)/shard_map/hand_on/pallas_call | solution.py:1247

commit v3 on v2

--- a/solution.py
+++ b/solution.py
@@ -405,106 +405,106 @@
 NAMES = ("aS", "aH0", "aH", "aK", "aO", "aR", "tS", "tH0", "tH", "tO", "tR")
 NAMES += ("P", "X", "N", "U", "L", "D", "C", "T2", "T1", "T", "W")
 ORDER = (
-    (6, 0, 0), (0, 0, 0), (0, 0, 1), (8, 0, 0, 1, 0), (1, 0, 0), (8, 0, 0, 1, 1), (2, 0, 0, 1, 0),
-    (2, 0, 0, 1, 1), (8, 0, 0, 2, 0), (12, 0), (7, 0, 0), (8, 0, 0, 2, 1), (2, 0, 1, 1, 0),
-    (2, 0, 1, 1, 1), (2, 0, 0, 2, 1), (3, 0, 0, 1, 1), (10, 0, 0, 0), (9, 0, 0, 1, 1),
-    (9, 0, 0, 1, 0), (2, 0, 0, 2, 0), (11, 0), (10, 0, 0, 1), (1, 0, 1), (12, 1), (9, 0, 0, 2, 1),
-    (3, 0, 0, 1, 0), (8, 0, 0, 3, 1), (9, 0, 0, 2, 0), (8, 0, 0, 3, 0), (0, 0, 3),
-    (9, 0, 0, 3, 1), (4, 0, 0, 1, 0), (2, 0, 0, 3, 1), (10, 0, 0, 2), (11, 1), (3, 0, 0, 2, 1),
-    (9, 0, 0, 3, 0), (4, 0, 1, 1, 0), (2, 0, 0, 3, 0), (3, 0, 0, 2, 0), (4, 0, 1, 1, 1),
-    (2, 0, 1, 2, 1), (12, 2), (2, 0, 1, 2, 0), (4, 0, 0, 2, 1), (3, 0, 1, 1, 1), (5, 0, 0, 0),
-    (10, 0, 0, 3), (3, 0, 1, 1, 0), (12, 3), (4, 0, 0, 2, 0), (4, 0, 0, 1, 1), (0, 0, 2), (11, 2),
-    (11, 3), (4, 0, 0, 3, 1), (2, 0, 3, 1, 0), (5, 0, 0, 1), (4, 0, 0, 3, 0), (3, 0, 0, 3, 0),
-    (2, 0, 3, 1, 1), (3, 0, 0, 3, 1), (14, 0, 0, 0), (14, 0, 0, 1), (5, 0, 0, 2), (5, 0, 1, 0),
-    (5, 0, 1, 1), (5, 0, 0, 3), (2, 0, 1, 3, 0), (14, 0, 0, 2), (14, 0, 1, 0), (2, 0, 1, 3, 1),
-    (14, 0, 0, 3), (3, 0, 1, 2, 1), (4, 0, 1, 2, 1), (3, 0, 1, 2, 0), (1, 0, 3), (15, 0, 0, 1),
-    (4, 0, 1, 2, 0), (14, 0, 1, 1), (15, 0, 0, 3), (13,), (5, 0, 1, 2), (4, 0, 1, 3, 0),
-    (4, 0, 1, 3, 1), (4, 0, 3, 1, 1), (16, 0, 0, 3, 1), (1, 0, 2), (16, 0, 0, 3, 0),
-    (15, 0, 0, 2), (2, 0, 2, 1, 1), (3, 0, 1, 3, 0), (2, 0, 2, 1, 0), (14, 0, 1, 2),
-    (2, 0, 3, 2, 1), (16, 0, 0, 2, 1), (3, 0, 1, 3, 1), (2, 0, 3, 2, 0), (16, 0, 0, 2, 0),
-    (15, 0, 1, 1), (3, 0, 3, 1, 1), (5, 0, 3, 0), (5, 0, 1, 3), (3, 0, 3, 1, 0), (17, 0, 0, 3, 0),
-    (17, 0, 0, 3, 1), (14, 0, 1, 3), (17, 0, 0, 2, 1), (3, 0, 2, 1, 1), (17, 0, 0, 2, 0),
-    (15, 0, 1, 3), (16, 0, 0, 1, 0), (5, 0, 2, 0), (14, 0, 3, 0), (16, 0, 1, 3, 1),
-    (2, 0, 2, 2, 1), (16, 0, 0, 1, 1), (2, 0, 3, 3, 0), (4, 0, 2, 1, 0), (4, 0, 3, 1, 0),
-    (3, 0, 3, 2, 0), (15, 0, 1, 2), (2, 0, 3, 3, 1), (2, 0, 2, 2, 0), (4, 0, 2, 1, 1),
-    (16, 0, 1, 3, 0), (16, 0, 1, 2, 1), (3, 0, 2, 1, 0), (16, 0, 1, 2, 0), (17, 0, 1, 3, 1),
-    (4, 0, 3, 2, 1), (5, 0, 3, 1), (17, 0, 1, 3, 0), (4, 0, 3, 3, 0), (3, 0, 3, 2, 1),
-    (17, 0, 0, 1, 0), (17, 0, 0, 1, 1), (4, 0, 3, 2, 0), (15, 0, 0, 0), (14, 0, 3, 1), (18, 0, 0),
-    (5, 0, 2, 1), (17, 0, 1, 2, 1), (4, 0, 3, 3, 1), (2, 0, 2, 3, 1), (5, 0, 3, 2),
-    (16, 0, 1, 1, 1), (3, 0, 2, 2, 0), (17, 0, 1, 2, 0), (3, 0, 2, 2, 1), (15, 0, 1, 0),
-    (14, 0, 3, 2), (16, 0, 1, 1, 0), (3, 0, 3, 3, 0), (14, 0, 2, 0), (2, 0, 2, 3, 0), (19, 0, 0),
-    (20, 0, 0), (3, 0, 3, 3, 1), (0, 1, 0), (5, 0, 3, 3), (14, 0, 3, 3), (3, 0, 2, 3, 1),
-    (15, 0, 3, 1), (17, 0, 1, 1, 1), (4, 0, 2, 2, 0), (17, 0, 1, 1, 0), (18, 0, 1), (1, 1, 0),
-    (15, 0, 3, 3), (5, 1, 0, 0), (4, 0, 2, 2, 1), (2, 1, 0, 1, 0), (16, 0, 3, 3, 0),
-    (2, 1, 0, 1, 1), (16, 0, 3, 3, 1), (3, 0, 2, 3, 0), (19, 0, 1), (4, 0, 2, 3, 1), (20, 0, 1),
-    (5, 0, 2, 2), (4, 0, 2, 3, 0), (0, 1, 1), (14, 0, 2, 1), (15, 0, 3, 2), (17, 0, 3, 3, 1),
-    (4, 1, 0, 1, 0), (17, 0, 3, 3, 0), (3, 1, 0, 1, 1), (14, 0, 2, 2), (5, 0, 2, 3),
-    (16, 0, 3, 2, 1), (2, 1, 0, 2, 1), (16, 0, 3, 2, 0), (3, 1, 0, 1, 0), (2, 1, 0, 2, 0),
-    (14, 0, 2, 3), (2, 1, 1, 1, 1), (2, 1, 1, 1, 0), (1, 1, 1), (15, 0, 2, 3), (16, 0, 2, 3, 0),
-    (16, 0, 3, 1, 1), (16, 0, 3, 1, 0), (16, 0, 2, 3, 1), (2, 1, 0, 3, 0), (3, 1, 0, 2, 1),
-    (15, 0, 3, 0), (5, 1, 1, 0), (4, 1, 0, 2, 0), (15, 0, 2, 2), (2, 1, 0, 3, 1),
-    (17, 0, 3, 2, 1), (4, 1, 0, 1, 1), (17, 0, 3, 2, 0), (2, 1, 1, 2, 1), (17, 0, 2, 3, 1),
-    (3, 1, 0, 2, 0), (4, 1, 0, 3, 0), (3, 1, 1, 1, 0), (4, 1, 0, 2, 1), (14, 1, 0, 0),
-    (17, 0, 2, 3, 0), (14, 1, 1, 0), (16, 0, 2, 2, 1), (5, 1, 0, 1), (2, 1, 1, 2, 0),
-    (4, 1, 1, 1, 1), (14, 1, 0, 1), (15, 0, 2, 1), (18, 0, 3), (3, 1, 1, 1, 1), (15, 0, 2, 0),
-    (5, 1, 0, 2), (16, 0, 2, 2, 0), (3, 1, 0, 3, 1), (17, 0, 3, 1, 0), (4, 1, 0, 3, 1),
-    (14, 1, 0, 2), (17, 0, 3, 1, 1), (3, 1, 0, 3, 0), (17, 0, 2, 2, 1), (17, 0, 2, 2, 0),
-    (5, 1, 0, 3), (16, 0, 2, 1, 0), (3, 1, 1, 2, 0), (3, 1, 1, 2, 1), (16, 0, 2, 1, 1),
-    (4, 1, 1, 1, 0), (2, 1, 1, 3, 1), (2, 1, 1, 3, 0), (14, 1, 0, 3), (19, 0, 3), (20, 0, 3),
-    (0, 1, 3), (3, 1, 1, 3, 1), (4, 1, 1, 3, 0), (17, 0, 2, 1, 1), (17, 0, 2, 1, 0),
-    (4, 1, 1, 3, 1), (5, 1, 1, 1), (18, 0, 2), (3, 1, 1, 3, 0), (4, 1, 1, 2, 0), (4, 1, 1, 2, 1),
-    (15, 1, 0, 3), (14, 1, 1, 1), (1, 1, 3), (5, 1, 1, 3), (16, 1, 0, 3, 1), (2, 1, 3, 1, 0),
-    (5, 1, 1, 2), (16, 1, 0, 3, 0), (14, 1, 1, 2), (2, 1, 3, 1, 1), (14, 1, 1, 3), (19, 0, 2),
-    (20, 0, 2), (0, 1, 2), (15, 1, 1, 3), (16, 1, 1, 3, 1), (16, 1, 1, 3, 0), (15, 1, 0, 2),
-    (3, 1, 3, 1, 0), (17, 1, 0, 3, 0), (15, 1, 1, 2), (4, 1, 3, 1, 0), (16, 1, 0, 2, 1),
-    (3, 1, 3, 1, 1), (17, 1, 0, 3, 1), (17, 1, 1, 3, 1), (4, 1, 3, 1, 1), (2, 1, 3, 2, 0),
-    (5, 1, 3, 0), (2, 1, 3, 2, 1), (17, 1, 1, 3, 0), (1, 1, 2), (16, 1, 1, 2, 1), (5, 1, 3, 1),
-    (14, 1, 3, 0), (16, 1, 0, 2, 0), (2, 1, 2, 1, 0), (16, 1, 1, 2, 0), (14, 1, 3, 1),
-    (2, 1, 2, 1, 1), (2, 1, 3, 3, 0), (17, 1, 1, 2, 0), (2, 1, 3, 3, 1), (15, 1, 1, 1),
-    (3, 1, 3, 2, 0), (17, 1, 1, 2, 1), (3, 1, 3, 2, 1), (4, 1, 3, 3, 1), (17, 1, 0, 2, 0),
-    (15, 1, 0, 1), (16, 1, 1, 1, 0), (4, 1, 3, 2, 1), (16, 1, 0, 1, 0), (4, 1, 3, 2, 0),
-    (4, 1, 3, 3, 0), (16, 1, 1, 1, 1), (3, 1, 3, 3, 0), (3, 1, 3, 3, 1), (2, 1, 2, 2, 1),
-    (17, 1, 0, 2, 1), (16, 1, 0, 1, 1), (5, 1, 3, 2), (2, 1, 2, 2, 0), (14, 1, 3, 2),
-    (5, 1, 3, 3), (17, 1, 1, 1, 1), (15, 1, 1, 0), (17, 1, 1, 1, 0), (15, 1, 0, 0),
-    (3, 1, 2, 1, 1), (4, 1, 2, 1, 1), (14, 1, 3, 3), (18, 1, 1), (15, 1, 3, 3), (16, 1, 3, 3, 0),
-    (16, 1, 3, 3, 1), (17, 1, 0, 1, 1), (2, 1, 2, 3, 1), (3, 1, 2, 1, 0), (18, 1, 0),
-    (17, 1, 0, 1, 0), (19, 1, 1), (20, 1, 1), (15, 1, 3, 2), (16, 1, 3, 2, 1), (17, 1, 3, 3, 1),
-    (3, 1, 2, 2, 0), (5, 1, 2, 0), (15, 1, 3, 1), (17, 1, 3, 3, 0), (3, 1, 2, 2, 1),
-    (2, 1, 2, 3, 0), (16, 1, 3, 2, 0), (4, 1, 2, 1, 0), (21, 1), (14, 1, 2, 0), (4, 1, 2, 2, 0),
-    (0, 2, 1), (5, 1, 2, 1), (4, 1, 2, 2, 1), (19, 1, 0), (20, 1, 0), (14, 1, 2, 1),
-    (16, 1, 3, 1, 1), (17, 1, 3, 2, 0), (15, 1, 3, 0), (4, 1, 2, 3, 1), (16, 1, 3, 1, 0),
-    (3, 1, 2, 3, 0), (4, 1, 2, 3, 0), (17, 1, 3, 2, 1), (5, 1, 2, 2), (3, 1, 2, 3, 1), (21, 0),
-    (0, 2, 0), (14, 1, 2, 2), (5, 1, 2, 3), (14, 1, 2, 3), (2, 2, 1, 1, 0), (2, 2, 1, 1, 1),
-    (17, 1, 3, 1, 0), (17, 1, 3, 1, 1), (15, 1, 2, 3), (16, 1, 2, 3, 1), (2, 2, 0, 1, 1),
-    (1, 2, 1), (17, 1, 2, 3, 1), (2, 2, 0, 1, 0), (15, 1, 2, 2), (18, 1, 3), (16, 1, 2, 3, 0),
-    (17, 1, 2, 3, 0), (15, 1, 2, 1), (5, 2, 1, 0), (16, 1, 2, 2, 1), (2, 2, 1, 2, 1),
-    (15, 1, 2, 0), (16, 1, 2, 2, 0), (4, 2, 1, 1, 1), (1, 2, 0), (2, 2, 1, 2, 0), (19, 1, 3),
-    (2, 2, 0, 2, 1), (17, 1, 2, 2, 1), (5, 2, 0, 0), (17, 1, 2, 2, 0), (3, 2, 1, 1, 1),
-    (2, 2, 1, 3, 1), (3, 2, 1, 1, 0), (4, 2, 1, 1, 0), (2, 2, 0, 2, 0), (20, 1, 3),
-    (4, 2, 0, 1, 1), (16, 1, 2, 1, 0), (3, 2, 0, 1, 1), (16, 1, 2, 1, 1), (3, 2, 0, 1, 0),
-    (17, 1, 2, 1, 0), (17, 1, 2, 1, 1), (14, 2, 1, 0), (21, 3), (0, 2, 3), (2, 2, 0, 3, 0),
-    (4, 2, 0, 1, 0), (18, 1, 2), (14, 2, 0, 0), (3, 2, 0, 2, 1), (4, 2, 1, 2, 0), (3, 2, 0, 2, 0),
-    (2, 2, 0, 3, 1), (4, 2, 0, 2, 0), (3, 2, 1, 2, 1), (5, 2, 0, 1), (19, 1, 2), (4, 2, 0, 3, 0),
-    (1, 2, 3), (20, 1, 2), (2, 2, 3, 1, 1), (3, 2, 0, 3, 0), (3, 2, 1, 2, 0), (2, 2, 3, 1, 0),
-    (21, 2), (3, 2, 3, 1, 1), (4, 2, 0, 2, 1), (4, 2, 1, 3, 1), (0, 2, 2), (5, 2, 1, 1),
-    (14, 2, 1, 1), (2, 2, 3, 2, 1), (5, 2, 0, 2), (14, 2, 0, 1), (3, 2, 3, 1, 0), (2, 2, 1, 3, 0),
-    (3, 2, 1, 3, 1), (3, 2, 0, 3, 1), (4, 2, 1, 2, 1), (2, 2, 3, 2, 0), (4, 2, 3, 1, 1),
-    (4, 2, 0, 3, 1), (5, 2, 3, 0), (2, 2, 2, 1, 1), (14, 2, 0, 2), (2, 2, 2, 1, 0),
-    (4, 2, 3, 1, 0), (5, 2, 0, 3), (2, 2, 3, 3, 0), (1, 2, 2), (3, 2, 1, 3, 0), (14, 2, 3, 0),
-    (5, 2, 3, 1), (4, 2, 1, 3, 0), (14, 2, 3, 1), (2, 2, 2, 2, 0), (2, 2, 3, 3, 1), (5, 2, 1, 3),
-    (4, 2, 3, 2, 1), (5, 2, 1, 2), (3, 2, 3, 2, 0), (2, 2, 2, 2, 1), (14, 2, 0, 3),
-    (2, 2, 2, 3, 1), (14, 2, 1, 2), (5, 2, 2, 0), (4, 2, 3, 3, 1), (3, 2, 2, 1, 1),
-    (4, 2, 3, 2, 0), (3, 2, 2, 1, 0), (4, 2, 2, 1, 0), (4, 2, 2, 1, 1), (3, 2, 3, 2, 1),
-    (4, 2, 3, 3, 0), (2, 2, 2, 3, 0), (14, 2, 2, 0), (14, 2, 1, 3), (3, 2, 3, 3, 0),
-    (3, 2, 3, 3, 1), (5, 2, 2, 1), (5, 2, 3, 2), (3, 2, 2, 2, 1), (3, 2, 2, 2, 0), (14, 2, 2, 1),
-    (14, 2, 3, 2), (5, 2, 3, 3), (4, 2, 2, 2, 0), (3, 2, 2, 3, 0), (4, 2, 2, 2, 1),
-    (4, 2, 2, 3, 0), (4, 2, 2, 3, 1), (3, 2, 2, 3, 1), (14, 2, 3, 3), (5, 2, 2, 2), (5, 2, 2, 3),
-    (14, 2, 2, 2), (14, 2, 2, 3),
+    (6, 0, 0), (13,), (0, 0, 0), (7, 0, 0), (0, 0, 1), (8, 0, 0, 1, 1), (12, 0), (8, 0, 0, 1, 0),
+    (1, 0, 0), (2, 0, 0, 1, 0), (8, 0, 0, 2, 0), (2, 0, 0, 1, 1), (8, 0, 0, 2, 1), (12, 1),
+    (12, 2), (2, 0, 1, 1, 1), (10, 0, 0, 0), (2, 0, 1, 1, 0), (3, 0, 0, 1, 0), (3, 0, 0, 1, 1),
+    (1, 0, 1), (4, 0, 0, 1, 1), (9, 0, 0, 2, 0), (8, 0, 0, 3, 0), (9, 0, 0, 1, 0),
+    (9, 0, 0, 2, 1), (9, 0, 0, 1, 1), (5, 0, 0, 0), (2, 0, 0, 2, 0), (8, 0, 0, 3, 1),
+    (2, 0, 0, 2, 1), (2, 0, 1, 2, 1), (11, 0), (2, 0, 1, 2, 0), (3, 0, 0, 2, 1), (9, 0, 0, 3, 1),
+    (3, 0, 0, 2, 0), (10, 0, 0, 1), (4, 0, 0, 1, 0), (12, 3), (5, 0, 1, 0), (0, 0, 2),
+    (3, 0, 1, 1, 0), (11, 1), (4, 0, 0, 2, 0), (3, 0, 1, 1, 1), (4, 0, 0, 2, 1), (2, 0, 0, 3, 0),
+    (4, 0, 1, 1, 1), (14, 0, 0, 0), (9, 0, 0, 3, 0), (10, 0, 0, 2), (5, 0, 0, 1), (2, 0, 0, 3, 1),
+    (0, 0, 3), (4, 0, 1, 1, 0), (14, 0, 0, 1), (2, 0, 1, 3, 1), (11, 2), (3, 0, 0, 3, 0),
+    (3, 0, 0, 3, 1), (2, 0, 1, 3, 0), (10, 0, 0, 3), (5, 0, 0, 2), (14, 0, 0, 2), (4, 0, 0, 3, 1),
+    (4, 0, 0, 3, 0), (11, 3), (15, 0, 0, 1), (5, 0, 0, 3), (14, 0, 0, 3), (4, 0, 1, 2, 1),
+    (3, 0, 1, 2, 1), (3, 0, 1, 2, 0), (4, 0, 1, 2, 0), (2, 0, 2, 1, 1), (2, 0, 2, 1, 0),
+    (1, 0, 2), (2, 0, 3, 1, 0), (15, 0, 0, 3), (16, 0, 0, 3, 1), (4, 0, 1, 3, 1), (1, 0, 3),
+    (14, 0, 1, 0), (5, 0, 1, 1), (3, 0, 1, 3, 1), (4, 0, 1, 3, 0), (5, 0, 1, 2), (16, 0, 0, 3, 0),
+    (15, 0, 0, 2), (3, 0, 1, 3, 0), (2, 0, 3, 1, 1), (14, 0, 1, 1), (5, 0, 1, 3), (4, 0, 2, 1, 1),
+    (4, 0, 2, 1, 0), (5, 0, 2, 0), (16, 0, 0, 2, 0), (16, 0, 0, 2, 1), (2, 0, 2, 2, 1),
+    (14, 0, 1, 2), (14, 0, 2, 0), (17, 0, 0, 3, 0), (14, 0, 1, 3), (3, 0, 2, 1, 1),
+    (2, 0, 2, 2, 0), (16, 0, 0, 1, 1), (3, 0, 2, 1, 0), (17, 0, 0, 3, 1), (15, 0, 0, 0),
+    (16, 0, 0, 1, 0), (4, 0, 3, 1, 0), (17, 0, 0, 2, 0), (15, 0, 1, 3), (2, 0, 3, 2, 1),
+    (5, 0, 3, 0), (5, 0, 2, 1), (2, 0, 3, 2, 0), (4, 0, 3, 1, 1), (17, 0, 0, 2, 1),
+    (3, 0, 3, 1, 1), (14, 0, 3, 0), (16, 0, 1, 3, 0), (16, 0, 1, 3, 1), (4, 0, 2, 2, 0),
+    (4, 0, 2, 2, 1), (14, 0, 2, 1), (2, 0, 2, 3, 1), (15, 0, 1, 2), (2, 0, 2, 3, 0),
+    (3, 0, 3, 1, 0), (16, 0, 1, 2, 0), (16, 0, 1, 2, 1), (17, 0, 1, 3, 0), (17, 0, 1, 3, 1),
+    (3, 0, 2, 2, 0), (15, 0, 1, 1), (3, 0, 2, 2, 1), (17, 0, 0, 1, 0), (17, 0, 0, 1, 1),
+    (5, 0, 2, 2), (18, 0, 0), (5, 0, 3, 1), (15, 0, 1, 0), (14, 0, 2, 2), (2, 0, 3, 3, 1),
+    (4, 0, 3, 2, 1), (17, 0, 1, 2, 1), (3, 0, 2, 3, 0), (15, 0, 2, 1), (4, 0, 2, 3, 0),
+    (2, 0, 3, 3, 0), (4, 0, 2, 3, 1), (17, 0, 1, 2, 0), (16, 0, 1, 1, 0), (3, 0, 2, 3, 1),
+    (3, 0, 3, 2, 0), (16, 0, 1, 1, 1), (3, 0, 3, 2, 1), (5, 0, 2, 3), (14, 0, 2, 3), (19, 0, 0),
+    (20, 0, 0), (0, 1, 0), (4, 0, 3, 3, 1), (4, 0, 3, 2, 0), (15, 0, 2, 3), (3, 0, 3, 3, 0),
+    (16, 0, 2, 3, 0), (17, 0, 1, 1, 0), (17, 0, 1, 1, 1), (16, 0, 2, 3, 1), (18, 0, 1),
+    (5, 0, 3, 2), (14, 0, 3, 1), (15, 0, 2, 2), (1, 1, 0), (16, 0, 2, 2, 0), (2, 1, 0, 1, 1),
+    (4, 0, 3, 3, 0), (2, 1, 0, 1, 0), (3, 0, 3, 3, 1), (5, 0, 3, 3), (17, 0, 2, 3, 0), (19, 0, 1),
+    (16, 0, 2, 2, 1), (20, 0, 1), (14, 0, 3, 2), (0, 1, 1), (14, 0, 3, 3), (3, 1, 0, 1, 0),
+    (5, 1, 0, 0), (2, 1, 0, 2, 0), (3, 1, 0, 1, 1), (2, 1, 0, 2, 1), (17, 0, 2, 2, 0),
+    (17, 0, 2, 3, 1), (4, 1, 0, 1, 0), (15, 0, 3, 3), (2, 1, 1, 1, 1), (15, 0, 2, 0),
+    (14, 1, 0, 0), (16, 0, 3, 3, 1), (1, 1, 1), (16, 0, 3, 3, 0), (4, 1, 0, 2, 1),
+    (3, 1, 0, 2, 1), (17, 0, 2, 2, 1), (16, 0, 2, 1, 0), (3, 1, 0, 2, 0), (4, 1, 0, 2, 0),
+    (2, 1, 1, 1, 0), (5, 1, 0, 2), (2, 1, 0, 3, 1), (16, 0, 2, 1, 1), (17, 0, 3, 3, 0),
+    (15, 0, 3, 2), (2, 1, 0, 3, 0), (17, 0, 3, 3, 1), (4, 1, 0, 1, 1), (16, 0, 3, 2, 1),
+    (16, 0, 3, 2, 0), (3, 1, 1, 1, 1), (15, 0, 3, 0), (17, 0, 2, 1, 0), (17, 0, 2, 1, 1),
+    (5, 1, 0, 1), (18, 0, 2), (3, 1, 0, 3, 1), (4, 1, 0, 3, 1), (3, 1, 1, 1, 0), (4, 1, 1, 1, 1),
+    (15, 0, 3, 1), (14, 1, 0, 1), (4, 1, 1, 1, 0), (3, 1, 0, 3, 0), (5, 1, 1, 0), (14, 1, 1, 0),
+    (2, 1, 1, 2, 1), (17, 0, 3, 2, 1), (17, 0, 3, 2, 0), (2, 1, 1, 2, 0), (4, 1, 0, 3, 0),
+    (16, 0, 3, 1, 0), (5, 1, 0, 3), (16, 0, 3, 1, 1), (14, 1, 0, 2), (14, 1, 0, 3),
+    (3, 1, 1, 2, 1), (3, 1, 1, 2, 0), (19, 0, 2), (20, 0, 2), (0, 1, 2), (15, 1, 0, 3),
+    (2, 1, 1, 3, 1), (2, 1, 1, 3, 0), (18, 0, 3), (17, 0, 3, 1, 0), (15, 1, 0, 2), (5, 1, 1, 1),
+    (3, 1, 1, 3, 0), (4, 1, 1, 2, 0), (17, 0, 3, 1, 1), (4, 1, 1, 2, 1), (14, 1, 1, 1),
+    (16, 1, 0, 3, 0), (16, 1, 0, 3, 1), (1, 1, 2), (2, 1, 2, 1, 0), (3, 1, 1, 3, 1),
+    (2, 1, 2, 1, 1), (17, 1, 0, 3, 0), (4, 1, 1, 3, 0), (4, 1, 1, 3, 1), (16, 1, 0, 2, 0),
+    (16, 1, 0, 2, 1), (5, 1, 1, 3), (19, 0, 3), (17, 1, 0, 3, 1), (5, 1, 1, 2), (14, 1, 1, 2),
+    (20, 0, 3), (0, 1, 3), (14, 1, 1, 3), (3, 1, 2, 1, 0), (4, 1, 2, 1, 0), (4, 1, 2, 1, 1),
+    (2, 1, 2, 2, 0), (2, 1, 2, 2, 1), (17, 1, 0, 2, 0), (15, 1, 1, 3), (16, 1, 1, 3, 1),
+    (3, 1, 2, 1, 1), (15, 1, 1, 2), (1, 1, 3), (17, 1, 0, 2, 1), (5, 1, 3, 0), (4, 1, 2, 2, 0),
+    (3, 1, 2, 2, 0), (5, 1, 2, 1), (16, 1, 1, 3, 0), (15, 1, 0, 1), (4, 1, 2, 2, 1),
+    (2, 1, 2, 3, 0), (16, 1, 0, 1, 0), (16, 1, 0, 1, 1), (2, 1, 3, 1, 0), (17, 1, 1, 3, 1),
+    (17, 1, 1, 3, 0), (3, 1, 2, 2, 1), (2, 1, 2, 3, 1), (15, 1, 0, 0), (5, 1, 2, 0),
+    (2, 1, 3, 1, 1), (14, 1, 2, 0), (14, 1, 2, 1), (17, 1, 0, 1, 1), (17, 1, 0, 1, 0),
+    (5, 1, 2, 2), (18, 1, 0), (3, 1, 2, 3, 1), (15, 1, 1, 1), (4, 1, 2, 3, 0), (3, 1, 3, 1, 1),
+    (14, 1, 3, 0), (14, 1, 2, 2), (4, 1, 2, 3, 1), (16, 1, 1, 2, 0), (3, 1, 2, 3, 0),
+    (16, 1, 1, 2, 1), (3, 1, 3, 1, 0), (17, 1, 1, 2, 0), (5, 1, 2, 3), (17, 1, 1, 2, 1),
+    (4, 1, 3, 1, 0), (2, 1, 3, 2, 0), (2, 1, 3, 2, 1), (14, 1, 2, 3), (19, 1, 0), (15, 1, 1, 0),
+    (4, 1, 3, 1, 1), (20, 1, 0), (3, 1, 3, 2, 1), (3, 1, 3, 2, 0), (16, 1, 1, 1, 0),
+    (15, 1, 2, 3), (16, 1, 2, 3, 0), (5, 1, 3, 1), (16, 1, 1, 1, 1), (17, 1, 1, 1, 0),
+    (16, 1, 2, 3, 1), (2, 1, 3, 3, 0), (2, 1, 3, 3, 1), (4, 1, 3, 2, 1), (4, 1, 3, 2, 0), (21, 0),
+    (0, 2, 0), (15, 1, 2, 2), (3, 1, 3, 3, 1), (14, 1, 3, 1), (3, 1, 3, 3, 0), (16, 1, 2, 2, 0),
+    (5, 1, 3, 2), (14, 1, 3, 2), (4, 1, 3, 3, 1), (18, 1, 1), (17, 1, 1, 1, 1), (17, 1, 2, 3, 0),
+    (15, 1, 2, 1), (17, 1, 2, 3, 1), (4, 1, 3, 3, 0), (16, 1, 2, 2, 1), (5, 1, 3, 3),
+    (14, 1, 3, 3), (1, 2, 0), (2, 2, 0, 1, 0), (2, 2, 0, 1, 1), (16, 1, 2, 1, 0), (19, 1, 1),
+    (20, 1, 1), (17, 1, 2, 2, 1), (15, 1, 3, 3), (16, 1, 3, 3, 0), (17, 1, 2, 2, 0),
+    (3, 2, 0, 1, 1), (16, 1, 3, 3, 1), (15, 1, 3, 2), (3, 2, 0, 1, 0), (16, 1, 2, 1, 1), (21, 1),
+    (2, 2, 0, 2, 1), (4, 2, 0, 1, 1), (2, 2, 0, 2, 0), (16, 1, 3, 2, 0), (17, 1, 3, 3, 0),
+    (15, 1, 2, 0), (4, 2, 0, 1, 0), (2, 2, 0, 3, 1), (0, 2, 1), (17, 1, 3, 3, 1), (3, 2, 0, 2, 0),
+    (18, 1, 2), (17, 1, 2, 1, 0), (16, 1, 3, 2, 1), (17, 1, 2, 1, 1), (3, 2, 0, 2, 1),
+    (15, 1, 3, 1), (4, 2, 0, 2, 1), (2, 2, 1, 1, 1), (17, 1, 3, 2, 1), (17, 1, 3, 2, 0),
+    (16, 1, 3, 1, 0), (15, 1, 3, 0), (2, 2, 1, 1, 0), (16, 1, 3, 1, 1), (5, 2, 0, 0),
+    (14, 2, 0, 0), (1, 2, 1), (19, 1, 2), (20, 1, 2), (2, 2, 1, 2, 1), (17, 1, 3, 1, 0),
+    (17, 1, 3, 1, 1), (5, 2, 1, 0), (18, 1, 3), (2, 2, 0, 3, 0), (21, 2), (0, 2, 2),
+    (2, 2, 1, 2, 0), (3, 2, 1, 1, 1), (3, 2, 1, 1, 0), (19, 1, 3), (20, 1, 3), (4, 2, 1, 1, 0),
+    (1, 2, 2), (5, 2, 0, 1), (3, 2, 1, 2, 0), (2, 2, 2, 1, 1), (2, 2, 1, 3, 0), (2, 2, 1, 3, 1),
+    (4, 2, 1, 1, 1), (14, 2, 1, 0), (4, 2, 0, 3, 0), (4, 2, 0, 2, 0), (4, 2, 1, 2, 0), (21, 3),
+    (0, 2, 3), (14, 2, 0, 1), (4, 2, 0, 3, 1), (5, 2, 2, 0), (2, 2, 2, 1, 0), (3, 2, 1, 2, 1),
+    (4, 2, 1, 3, 1), (14, 2, 2, 0), (5, 2, 1, 1), (14, 2, 1, 1), (3, 2, 0, 3, 1), (2, 2, 2, 2, 1),
+    (4, 2, 1, 3, 0), (3, 2, 0, 3, 0), (4, 2, 2, 1, 1), (2, 2, 3, 1, 0), (4, 2, 1, 2, 1),
+    (2, 2, 2, 3, 1), (2, 2, 3, 1, 1), (3, 2, 1, 3, 1), (1, 2, 3), (4, 2, 2, 1, 0), (5, 2, 0, 2),
+    (2, 2, 3, 2, 1), (2, 2, 2, 2, 0), (3, 2, 2, 1, 1), (5, 2, 1, 2), (14, 2, 0, 2),
+    (2, 2, 3, 2, 0), (5, 2, 0, 3), (3, 2, 2, 1, 0), (3, 2, 1, 3, 0), (5, 2, 3, 0), (14, 2, 1, 2),
+    (4, 2, 3, 1, 0), (14, 2, 0, 3), (3, 2, 3, 1, 1), (5, 2, 2, 1), (14, 2, 2, 1), (5, 2, 1, 3),
+    (2, 2, 2, 3, 0), (2, 2, 3, 3, 1), (4, 2, 2, 2, 1), (4, 2, 3, 1, 1), (14, 2, 3, 0),
+    (3, 2, 3, 1, 0), (4, 2, 2, 2, 0), (14, 2, 1, 3), (3, 2, 2, 2, 1), (3, 2, 3, 2, 1),
+    (4, 2, 3, 2, 0), (4, 2, 2, 3, 1), (4, 2, 3, 2, 1), (2, 2, 3, 3, 0), (3, 2, 2, 2, 0),
+    (5, 2, 3, 1), (3, 2, 2, 3, 1), (14, 2, 3, 1), (4, 2, 2, 3, 0), (3, 2, 2, 3, 0),
+    (3, 2, 3, 2, 0), (5, 2, 2, 2), (3, 2, 3, 3, 0), (5, 2, 3, 2), (14, 2, 3, 2), (3, 2, 3, 3, 1),
+    (5, 2, 2, 3), (4, 2, 3, 3, 1), (4, 2, 3, 3, 0), (14, 2, 2, 2), (14, 2, 2, 3), (5, 2, 3, 3),
+    (14, 2, 3, 3),
 )
 ROUTE = ("S", "H0", "H", "K", "O", "R")
 CHAINS = 1 + max(step[2] for step in ORDER if NAMES[step[0]] == "aS")
 PLANES = 1 + max(step[3] for step in ORDER if NAMES[step[0]] == "U")
-GATHER_SPLIT = ((13, 11, 10, 10), (9, 9, 9, 9), (10, 10, 11, 13))
+GATHER_SPLIT = ((12, 10, 10, 10), (10, 10, 10, 10), (10, 10, 10, 12))
 SCATTER_SPLIT = ((10, 10, 10, 10), (10, 10, 10, 10))
 
 

time: 195 us -> 194 us (level)
  no operation moved by 1% of the time
where the time goes in v3:
time: 194 us
  Pallas kernels  193 us (99%)
    pallas_call x1, Pallas kernels, fused(): pl.pallas_call(functools.partial(fused_kernel, plan), out_shape=[jax.Shap...  190 us

profile of v3, /device:TPU:0, one launch (start us, length us, event | category | flops | bytes accessed | tf_op | source)
XLA Modules:
  0.0 193.7 jit_solution(18109480482400413599)
XLA Ops:
  0.6 190.4 %fused.1 = (bf16[128,2048]{1,0:T(8,128)(2,1)}, bf16[1024,768]{1,0:T(8,128)(2,1)}) custom-call(bf16[128,2048]{1,0:T(8,128)(2,1)} %cot.1, s32[6,128]{1,0:T(8,128)} %bitcast.10, f32[6,128]{1,0:T(8,128)} %bitcast.11, bf16[896,768]{1,0:T(8,128)(2,1)} %bitcast.9, bf16[2048,768]{1,0:T(8,128)(2,1)} %bitcast.6, bf16[2048,768]{1,0:T(8,128)(2,1)} %bitcast.7), custom_call_target="tpu_custom_call" | custom-call | flops 40000000000 | bytes 20000000 | tf_op jit(solution)/shard_map/fused/pallas_call | solution.py:1176
  191.0 2.5 %hand_on.1 = (bf16[128,2048]{1,0:T(8,128)(2,1)}, bf16[1024,768]{1,0:T(8,128)(2,1)}) custom-call(bf16[128,2048]{1,0:T(8,128)(2,1)} %get-tuple-element.6.refs_0_, bf16[1024,768]{1,0:T(8,128)(2,1)} %get-tuple-element.7.refs_1_), custom_call_target="tpu_custom_call" | custom-call | tf_op jit(solution)/shard_map/hand_on/pallas_call | solution.py:1247
